TPU v7x, 256 devices: a whole 4x4x8 slice. The times are simulated.
256 devices in a mesh: cp: 64 (over z, x, core), tp: 4 (over y).
Axes of the slice: x: 4, y: 4, z: 8, core: 2. Of those that a mesh axis runs over, the one named last changes fastest.
Arguments:
- queries: bfloat16 [8192, 8192], P('cp', 'tp'), may hold values from -6 to 6
- keys: bfloat16 [8192, 1024], P('cp', 'tp'), may hold values from -6 to 6
- values: bfloat16 [8192, 1024], P('cp', 'tp'), may hold values from -6 to 6
- doc_blocks: int32 [4], replicated, may hold values from 1 to 32, 64 in all
- block_order: int32 [64], replicated, may hold values from 0 to 63, each once
- out_weight: bfloat16 [8192, 4096], P('tp'), may hold values from -0.5 to 0.5
Outputs:
- layer_out: bfloat16 [8192, 4096], P(('cp', 'tp'))
Inputs may be any that keep to these rules, and one draw needn't show every extreme that they name: Array block i (rows i * 128 to i * 128 + 127) holds sequence block block_order[i]; every block number appears once. `doc_blocks`: they sum to 64; the longest document has exactly 32 blocks.
All inputs are finite; a program needn't handle non-finite values.
Results may differ from a plain program's by a relative error of at most 0.013.
Values may be sent and summed in bfloat16 or wider, within the bound.
A program may use at most 128 MiB of HBM per device.

v0:
```python
import jax
import jax.numpy as jnp
from jax import lax
from jax.sharding import PartitionSpec as P

HEAD_SIZE = 128
BLOCK_TOKENS = 128


document_masked_score = -1e30


def in_one_piece(arrays, axis, dim, along):
    both = jnp.concatenate(arrays, axis=along)
    result, at, gathered = (lax.all_gather(both, axis, axis=dim, tiled=True), 0, [])
    for a in arrays:
        gathered.append(lax.slice_in_dim(result, at, at + a.shape[along], axis=along))
        at += a.shape[along]
    return tuple(gathered)


def cut_along(value, dim, length):
    before, after = (value.shape[:dim], value.shape[dim + 1 :])
    return jnp.moveaxis(value.reshape(*before, length, -1, *after), dim, 0)


def sent_and_summed(value, axis, dim):
    length = lax.axis_size(axis)
    parts = lax.all_to_all(cut_along(value, dim, length), axis, 0, 0, tiled=True)
    return jnp.sum(parts.astype(jnp.float32), axis=0)


def lookup(entries, indices):
    matches = indices[:, None] == jnp.arange(entries.shape[0], dtype=jnp.int32)[None, :]
    return jnp.sum(jnp.where(matches, entries[None, :], 0), axis=1)


def locate(row_ids, block_order, doc_ends):
    seq_block = lookup(block_order, row_ids // BLOCK_TOKENS)
    position = seq_block * BLOCK_TOKENS + row_ids % BLOCK_TOKENS
    doc_ids = jnp.sum((seq_block[:, None] >= doc_ends[None, :]).astype(jnp.int32), axis=1)
    return (position, doc_ids)


def attend(online, key_rows, value_rows, key_pos, key_doc, query_rows, query_pos, query_doc):
    allowed = (query_doc[:, None] == key_doc[None, :]) & (key_pos[None, :] <= query_pos[:, None])

    def compute(status):
        running_max, weight_sum, weighted = status
        scores = jnp.einsum(
            "qhgd,khd->hgqk", query_rows, key_rows, preferred_element_type=jnp.float32
        ) * HEAD_SIZE ** (-0.5)
        scores = jnp.where(allowed, scores, document_masked_score)
        new_max = jnp.maximum(running_max, jnp.max(scores, axis=-1))
        weights = jnp.where(allowed, jnp.exp(scores - new_max[..., None]), 0.0)
        factor = jnp.exp(running_max - new_max)
        weight_sum = weight_sum * factor + jnp.sum(weights, axis=-1)
        weighted = weighted * factor[..., None] + jnp.einsum(
            "hgqk,khd->hgqd",
            weights.astype(jnp.bfloat16),
            value_rows,
            preferred_element_type=jnp.float32,
        )
        return (new_max, weight_sum, weighted)

    return lax.cond(jnp.any(allowed), compute, lambda unchanged: unchanged, online)


def sweep_keys(
    online, key_part, value_part, block_order, doc_ends, query_rows, query_pos, query_doc
):
    length = key_part.shape[0]
    heads_kv = key_part.shape[1] // HEAD_SIZE
    block_rows = 512
    token_blocks = length // block_rows
    key_pos, key_doc = locate(jnp.arange(length, dtype=jnp.int32), block_order, doc_ends)

    def scan_step(status, pieces_now):
        return (
            attend(
                status,
                pieces_now[0],
                pieces_now[1],
                pieces_now[2],
                pieces_now[3],
                query_rows,
                query_pos,
                query_doc,
            ),
            None,
        )

    online, unused = lax.scan(
        scan_step,
        online,
        (
            key_part.reshape(token_blocks, block_rows, heads_kv, HEAD_SIZE),
            value_part.reshape(token_blocks, block_rows, heads_kv, HEAD_SIZE),
            key_pos.reshape(token_blocks, block_rows),
            key_doc.reshape(token_blocks, block_rows),
        ),
    )
    return online


def local(queries, keys, values, doc_blocks, block_order, out_weight):
    rows_dev = queries.shape[0]
    heads_kv = keys.shape[1] // HEAD_SIZE
    group_size = queries.shape[1] // keys.shape[1]
    doc_ends = jnp.cumsum(doc_blocks)
    first_row = lax.axis_index("cp") * rows_dev
    query_pos, query_doc = locate(
        first_row + jnp.arange(rows_dev, dtype=jnp.int32), block_order, doc_ends
    )
    query_rows = queries.reshape(rows_dev, heads_kv, group_size, HEAD_SIZE)
    starting_state = (
        jnp.full((heads_kv, group_size, rows_dev), document_masked_score, jnp.float32),
        jnp.zeros((heads_kv, group_size, rows_dev), jnp.float32),
        jnp.zeros((heads_kv, group_size, rows_dev, HEAD_SIZE), jnp.float32),
    )
    whole_keys, whole_values = in_one_piece((keys, values), "cp", 0, 1)
    running_max, weight_sum, weighted = sweep_keys(
        starting_state,
        whole_keys,
        whole_values,
        block_order,
        doc_ends,
        query_rows,
        query_pos,
        query_doc,
    )
    attended = (
        jnp.transpose(weighted / weight_sum[..., None], (2, 0, 1, 3))
        .reshape(rows_dev, -1)
        .astype(jnp.bfloat16)
    )
    summed = sent_and_summed(
        jnp.dot(attended, out_weight, preferred_element_type=jnp.float32).astype(jnp.bfloat16),
        "tp",
        0,
    )
    return summed.astype(jnp.bfloat16)


def solution(mesh):
    placed = (P("cp", "tp"), P("cp", "tp"), P("cp", "tp"), P(), P(), P("tp", None))
    return jax.shard_map(
        local, mesh=mesh, in_specs=placed, out_specs=P(("cp", "tp"), None), check_vma=False
    )
```

profile of v0, /device:TPU:68, one launch (start us, length us, event | category | flops | bytes accessed | tf_op | source)
XLA Modules:
  0.0 264.1 jit_solution(7884721170737599241)
XLA Ops:
  12.7 79.8 %all-gather.2.cloned.1.call-done = bf16[8192,512]{1,0:T(8,128)(2,1)} async-done(((bf16[128,512]{1,0:T(8,128)(2,1)}), bf16[8192,512]{1,0:T(8,128)(2,1)}) %all-gather.2.cloned.1.call-update) | async-done | bytes 8388624 | tf_op jit(solution)/shard_map/all_gather | solution.py:15
  92.5 5.7 %fusion.26 = (bf16[8192,256]{1,0:T(8,128)(2,1)}, bf16[8192,256]{1,0:T(8,128)(2,1)}) fusion(bf16[8192,512]{1,0:T(8,128)(2,1)} %all-gather.2.cloned.1.call-done), kind=kLoop, calls=%fused_computation.53 | loop fusion | bytes 16777216 | tf_op jit(solution)/shard_map/slice | solution.py:17
  98.2 6.9 %reshape.95 = bf16[16,512,2,128]{3,2,1,0:T(2,128)(2,1)} reshape(bf16[8192,256]{1,0:T(8,128)(2,1)} %get-tuple-element.194) | data formatting | bytes 8388608 | tf_op jit(solution)/shard_map/reshape | solution.py:97
  105.1 5.1 %copy.20 = bf16[16,512,2,128]{3,1,2,0:T(8,128)(2,1)} copy(bf16[16,512,2,128]{3,2,1,0:T(2,128)(2,1)} %reshape.95) | data formatting | bytes 8388608 | tf_op jit(solution)/shard_map/while | solution.py:93
  110.2 6.9 %reshape.96 = bf16[16,512,2,128]{3,2,1,0:T(2,128)(2,1)} reshape(bf16[8192,256]{1,0:T(8,128)(2,1)} %get-tuple-element.193) | data formatting | bytes 8388608 | tf_op jit(solution)/shard_map/reshape | solution.py:98
  117.1 5.2 %copy.22 = bf16[16,512,2,128]{3,1,2,0:T(8,128)(2,1)} copy(bf16[16,512,2,128]{3,2,1,0:T(2,128)(2,1)} %reshape.96) | data formatting | bytes 8388608 | tf_op jit(solution)/shard_map/while | solution.py:93
  122.4 105.7 %while.14 = (s32[]{:T(128)}, f32[2,8,128]{2,1,0:T(8,128)S(1)}, f32[2,8,128]{2,1,0:T(8,128)S(1)}, f32[2,8,128,128]{3,2,1,0:T(8,128)S(1)}, s32[128]{0:T(128)S(1)},...) while((s32[]{:T(128)}, f32[2,8,128]{2,1,0:T(8,128)S(1)}, ...), condition=%wide.region_11.12_spmd, body=%wide.region_5.11_spmd.sunk | while | flops 551292928 | bytes 16136439 | solution.py:93
  123.9 5.4 %conditional.2 = ((f32[2,8,128]{2,1,0:T(8,128)S(1)}, f32[2,8,128]{2,1,0:T(8,128)S(1)}, f32[2,8,128,128]{3,2,1,0:T(8,128)S(1)})) conditional(s32[]{:T(128)} %convert_element_type.43, (f32[2,8,128]{2,1,0:T(8,128)S(1)}, f32[2,8,128]{2,1,0:T(8,128)S(1)}, f32[2,8,128,128]{3,2,1,0:T(8,128)S(1)}) %tuple.42, (pred[128,512]{0,1:T(8,128)(4,1)S(1)}, ...), branch_computations={%region_7.7_spmd, %region_8.10_spmd} | conditional | flops 551030784 | bytes 16057376 | solution.py:66
  123.9 1.7 fusion
  126.7 2.6 %fusion.6 = f32[2,8,128,128]{3,2,1,0:T(8,128)S(1)} fusion(f32[2,512,128,8]{2,1,3,0:T(8,128)S(1)} %get-tuple-element.190, f32[2,8,128]{2,1,0:T(8,128)S(1)} %max.4, pred[128,512]{0,1:T(8,128)(4,1)S(1)} %get-tuple-element.115, f32[2,8,128,128]{3,2,1,0:T(8,128)S(1)} %get-tuple-element.120, f32[2,8,128]{2,1,0:T(8,128)S(1)} %get-tuple-element.186, ...), kind=kOutput, calls=%fused_computation.7 | convolution fusion | flops 274202624 | bytes 6636032 | tf_op jit(solution)/shard_map/while/body/eval_jaxpr/cond/branch_1_fun/hgqk,khd->hgqd/dot_general | solution.py:58
  130.9 5.4 %conditional.2 = ((f32[2,8,128]{2,1,0:T(8,128)S(1)}, f32[2,8,128]{2,1,0:T(8,128)S(1)}, f32[2,8,128,128]{3,2,1,0:T(8,128)S(1)})) conditional(s32[]{:T(128)} %convert_element_type.43, (f32[2,8,128]{2,1,0:T(8,128)S(1)}, f32[2,8,128]{2,1,0:T(8,128)S(1)}, f32[2,8,128,128]{3,2,1,0:T(8,128)S(1)}) %tuple.42, (pred[128,512]{0,1:T(8,128)(4,1)S(1)}, ...), branch_computations={%region_7.7_spmd, %region_8.10_spmd} | conditional | flops 551030784 | bytes 16057376 | solution.py:66
  133.6 2.7 %fusion.6 = f32[2,8,128,128]{3,2,1,0:T(8,128)S(1)} fusion(f32[2,512,128,8]{2,1,3,0:T(8,128)S(1)} %get-tuple-element.190, f32[2,8,128]{2,1,0:T(8,128)S(1)} %max.4, pred[128,512]{0,1:T(8,128)(4,1)S(1)} %get-tuple-element.115, f32[2,8,128,128]{3,2,1,0:T(8,128)S(1)} %get-tuple-element.120, f32[2,8,128]{2,1,0:T(8,128)S(1)} %get-tuple-element.186, ...), kind=kOutput, calls=%fused_computation.7 | convolution fusion | flops 274202624 | bytes 6636032 | tf_op jit(solution)/shard_map/while/body/eval_jaxpr/cond/branch_1_fun/hgqk,khd->hgqd/dot_general | solution.py:58
  137.8 5.4 %conditional.2 = ((f32[2,8,128]{2,1,0:T(8,128)S(1)}, f32[2,8,128]{2,1,0:T(8,128)S(1)}, f32[2,8,128,128]{3,2,1,0:T(8,128)S(1)})) conditional(s32[]{:T(128)} %convert_element_type.43, (f32[2,8,128]{2,1,0:T(8,128)S(1)}, f32[2,8,128]{2,1,0:T(8,128)S(1)}, f32[2,8,128,128]{3,2,1,0:T(8,128)S(1)}) %tuple.42, (pred[128,512]{0,1:T(8,128)(4,1)S(1)}, ...), branch_computations={%region_7.7_spmd, %region_8.10_spmd} | conditional | flops 551030784 | bytes 16057376 | solution.py:66
  137.8 1.7 fusion
  140.6 2.6 %fusion.6 = f32[2,8,128,128]{3,2,1,0:T(8,128)S(1)} fusion(f32[2,512,128,8]{2,1,3,0:T(8,128)S(1)} %get-tuple-element.190, f32[2,8,128]{2,1,0:T(8,128)S(1)} %max.4, pred[128,512]{0,1:T(8,128)(4,1)S(1)} %get-tuple-element.115, f32[2,8,128,128]{3,2,1,0:T(8,128)S(1)} %get-tuple-element.120, f32[2,8,128]{2,1,0:T(8,128)S(1)} %get-tuple-element.186, ...), kind=kOutput, calls=%fused_computation.7 | convolution fusion | flops 274202624 | bytes 6636032 | tf_op jit(solution)/shard_map/while/body/eval_jaxpr/cond/branch_1_fun/hgqk,khd->hgqd/dot_general | solution.py:58
  144.8 5.4 %conditional.2 = ((f32[2,8,128]{2,1,0:T(8,128)S(1)}, f32[2,8,128]{2,1,0:T(8,128)S(1)}, f32[2,8,128,128]{3,2,1,0:T(8,128)S(1)})) conditional(s32[]{:T(128)} %convert_element_type.43, (f32[2,8,128]{2,1,0:T(8,128)S(1)}, f32[2,8,128]{2,1,0:T(8,128)S(1)}, f32[2,8,128,128]{3,2,1,0:T(8,128)S(1)}) %tuple.42, (pred[128,512]{0,1:T(8,128)(4,1)S(1)}, ...), branch_computations={%region_7.7_spmd, %region_8.10_spmd} | conditional | flops 551030784 | bytes 16057376 | solution.py:66
  144.8 1.7 fusion
  147.5 2.6 %fusion.6 = f32[2,8,128,128]{3,2,1,0:T(8,128)S(1)} fusion(f32[2,512,128,8]{2,1,3,0:T(8,128)S(1)} %get-tuple-element.190, f32[2,8,128]{2,1,0:T(8,128)S(1)} %max.4, pred[128,512]{0,1:T(8,128)(4,1)S(1)} %get-tuple-element.115, f32[2,8,128,128]{3,2,1,0:T(8,128)S(1)} %get-tuple-element.120, f32[2,8,128]{2,1,0:T(8,128)S(1)} %get-tuple-element.186, ...), kind=kOutput, calls=%fused_computation.7 | convolution fusion | flops 274202624 | bytes 6636032 | tf_op jit(solution)/shard_map/while/body/eval_jaxpr/cond/branch_1_fun/hgqk,khd->hgqd/dot_general | solution.py:58
  151.7 5.4 %conditional.2 = ((f32[2,8,128]{2,1,0:T(8,128)S(1)}, f32[2,8,128]{2,1,0:T(8,128)S(1)}, f32[2,8,128,128]{3,2,1,0:T(8,128)S(1)})) conditional(s32[]{:T(128)} %convert_element_type.43, (f32[2,8,128]{2,1,0:T(8,128)S(1)}, f32[2,8,128]{2,1,0:T(8,128)S(1)}, f32[2,8,128,128]{3,2,1,0:T(8,128)S(1)}) %tuple.42, (pred[128,512]{0,1:T(8,128)(4,1)S(1)}, ...), branch_computations={%region_7.7_spmd, %region_8.10_spmd} | conditional | flops 551030784 | bytes 16057376 | solution.py:66
  154.5 2.7 %fusion.6 = f32[2,8,128,128]{3,2,1,0:T(8,128)S(1)} fusion(f32[2,512,128,8]{2,1,3,0:T(8,128)S(1)} %get-tuple-element.190, f32[2,8,128]{2,1,0:T(8,128)S(1)} %max.4, pred[128,512]{0,1:T(8,128)(4,1)S(1)} %get-tuple-element.115, f32[2,8,128,128]{3,2,1,0:T(8,128)S(1)} %get-tuple-element.120, f32[2,8,128]{2,1,0:T(8,128)S(1)} %get-tuple-element.186, ...), kind=kOutput, calls=%fused_computation.7 | convolution fusion | flops 274202624 | bytes 6636032 | tf_op jit(solution)/shard_map/while/body/eval_jaxpr/cond/branch_1_fun/hgqk,khd->hgqd/dot_general | solution.py:58
  158.6 5.4 %conditional.2 = ((f32[2,8,128]{2,1,0:T(8,128)S(1)}, f32[2,8,128]{2,1,0:T(8,128)S(1)}, f32[2,8,128,128]{3,2,1,0:T(8,128)S(1)})) conditional(s32[]{:T(128)} %convert_element_type.43, (f32[2,8,128]{2,1,0:T(8,128)S(1)}, f32[2,8,128]{2,1,0:T(8,128)S(1)}, f32[2,8,128,128]{3,2,1,0:T(8,128)S(1)}) %tuple.42, (pred[128,512]{0,1:T(8,128)(4,1)S(1)}, ...), branch_computations={%region_7.7_spmd, %region_8.10_spmd} | conditional | flops 551030784 | bytes 16057376 | solution.py:66
  158.7 1.7 fusion
  161.4 2.6 %fusion.6 = f32[2,8,128,128]{3,2,1,0:T(8,128)S(1)} fusion(f32[2,512,128,8]{2,1,3,0:T(8,128)S(1)} %get-tuple-element.190, f32[2,8,128]{2,1,0:T(8,128)S(1)} %max.4, pred[128,512]{0,1:T(8,128)(4,1)S(1)} %get-tuple-element.115, f32[2,8,128,128]{3,2,1,0:T(8,128)S(1)} %get-tuple-element.120, f32[2,8,128]{2,1,0:T(8,128)S(1)} %get-tuple-element.186, ...), kind=kOutput, calls=%fused_computation.7 | convolution fusion | flops 274202624 | bytes 6636032 | tf_op jit(solution)/shard_map/while/body/eval_jaxpr/cond/branch_1_fun/hgqk,khd->hgqd/dot_general | solution.py:58
  165.6 5.4 %conditional.2 = ((f32[2,8,128]{2,1,0:T(8,128)S(1)}, f32[2,8,128]{2,1,0:T(8,128)S(1)}, f32[2,8,128,128]{3,2,1,0:T(8,128)S(1)})) conditional(s32[]{:T(128)} %convert_element_type.43, (f32[2,8,128]{2,1,0:T(8,128)S(1)}, f32[2,8,128]{2,1,0:T(8,128)S(1)}, f32[2,8,128,128]{3,2,1,0:T(8,128)S(1)}) %tuple.42, (pred[128,512]{0,1:T(8,128)(4,1)S(1)}, ...), branch_computations={%region_7.7_spmd, %region_8.10_spmd} | conditional | flops 551030784 | bytes 16057376 | solution.py:66
  165.6 1.7 fusion
  168.3 2.6 %fusion.6 = f32[2,8,128,128]{3,2,1,0:T(8,128)S(1)} fusion(f32[2,512,128,8]{2,1,3,0:T(8,128)S(1)} %get-tuple-element.190, f32[2,8,128]{2,1,0:T(8,128)S(1)} %max.4, pred[128,512]{0,1:T(8,128)(4,1)S(1)} %get-tuple-element.115, f32[2,8,128,128]{3,2,1,0:T(8,128)S(1)} %get-tuple-element.120, f32[2,8,128]{2,1,0:T(8,128)S(1)} %get-tuple-element.186, ...), kind=kOutput, calls=%fused_computation.7 | convolution fusion | flops 274202624 | bytes 6636032 | tf_op jit(solution)/shard_map/while/body/eval_jaxpr/cond/branch_1_fun/hgqk,khd->hgqd/dot_general | solution.py:58
  172.5 5.4 %conditional.2 = ((f32[2,8,128]{2,1,0:T(8,128)S(1)}, f32[2,8,128]{2,1,0:T(8,128)S(1)}, f32[2,8,128,128]{3,2,1,0:T(8,128)S(1)})) conditional(s32[]{:T(128)} %convert_element_type.43, (f32[2,8,128]{2,1,0:T(8,128)S(1)}, f32[2,8,128]{2,1,0:T(8,128)S(1)}, f32[2,8,128,128]{3,2,1,0:T(8,128)S(1)}) %tuple.42, (pred[128,512]{0,1:T(8,128)(4,1)S(1)}, ...), branch_computations={%region_7.7_spmd, %region_8.10_spmd} | conditional | flops 551030784 | bytes 16057376 | solution.py:66
  175.3 2.7 %fusion.6 = f32[2,8,128,128]{3,2,1,0:T(8,128)S(1)} fusion(f32[2,512,128,8]{2,1,3,0:T(8,128)S(1)} %get-tuple-element.190, f32[2,8,128]{2,1,0:T(8,128)S(1)} %max.4, pred[128,512]{0,1:T(8,128)(4,1)S(1)} %get-tuple-element.115, f32[2,8,128,128]{3,2,1,0:T(8,128)S(1)} %get-tuple-element.120, f32[2,8,128]{2,1,0:T(8,128)S(1)} %get-tuple-element.186, ...), kind=kOutput, calls=%fused_computation.7 | convolution fusion | flops 274202624 | bytes 6636032 | tf_op jit(solution)/shard_map/while/body/eval_jaxpr/cond/branch_1_fun/hgqk,khd->hgqd/dot_general | solution.py:58
  179.5 5.4 %conditional.2 = ((f32[2,8,128]{2,1,0:T(8,128)S(1)}, f32[2,8,128]{2,1,0:T(8,128)S(1)}, f32[2,8,128,128]{3,2,1,0:T(8,128)S(1)})) conditional(s32[]{:T(128)} %convert_element_type.43, (f32[2,8,128]{2,1,0:T(8,128)S(1)}, f32[2,8,128]{2,1,0:T(8,128)S(1)}, f32[2,8,128,128]{3,2,1,0:T(8,128)S(1)}) %tuple.42, (pred[128,512]{0,1:T(8,128)(4,1)S(1)}, ...), branch_computations={%region_7.7_spmd, %region_8.10_spmd} | conditional | flops 551030784 | bytes 16057376 | solution.py:66
  179.5 1.7 fusion
  182.2 2.6 %fusion.6 = f32[2,8,128,128]{3,2,1,0:T(8,128)S(1)} fusion(f32[2,512,128,8]{2,1,3,0:T(8,128)S(1)} %get-tuple-element.190, f32[2,8,128]{2,1,0:T(8,128)S(1)} %max.4, pred[128,512]{0,1:T(8,128)(4,1)S(1)} %get-tuple-element.115, f32[2,8,128,128]{3,2,1,0:T(8,128)S(1)} %get-tuple-element.120, f32[2,8,128]{2,1,0:T(8,128)S(1)} %get-tuple-element.186, ...), kind=kOutput, calls=%fused_computation.7 | convolution fusion | flops 274202624 | bytes 6636032 | tf_op jit(solution)/shard_map/while/body/eval_jaxpr/cond/branch_1_fun/hgqk,khd->hgqd/dot_general | solution.py:58
  186.4 5.4 %conditional.2 = ((f32[2,8,128]{2,1,0:T(8,128)S(1)}, f32[2,8,128]{2,1,0:T(8,128)S(1)}, f32[2,8,128,128]{3,2,1,0:T(8,128)S(1)})) conditional(s32[]{:T(128)} %convert_element_type.43, (f32[2,8,128]{2,1,0:T(8,128)S(1)}, f32[2,8,128]{2,1,0:T(8,128)S(1)}, f32[2,8,128,128]{3,2,1,0:T(8,128)S(1)}) %tuple.42, (pred[128,512]{0,1:T(8,128)(4,1)S(1)}, ...), branch_computations={%region_7.7_spmd, %region_8.10_spmd} | conditional | flops 551030784 | bytes 16057376 | solution.py:66
  186.4 1.7 fusion
  189.2 2.6 %fusion.6 = f32[2,8,128,128]{3,2,1,0:T(8,128)S(1)} fusion(f32[2,512,128,8]{2,1,3,0:T(8,128)S(1)} %get-tuple-element.190, f32[2,8,128]{2,1,0:T(8,128)S(1)} %max.4, pred[128,512]{0,1:T(8,128)(4,1)S(1)} %get-tuple-element.115, f32[2,8,128,128]{3,2,1,0:T(8,128)S(1)} %get-tuple-element.120, f32[2,8,128]{2,1,0:T(8,128)S(1)} %get-tuple-element.186, ...), kind=kOutput, calls=%fused_computation.7 | convolution fusion | flops 274202624 | bytes 6636032 | tf_op jit(solution)/shard_map/while/body/eval_jaxpr/cond/branch_1_fun/hgqk,khd->hgqd/dot_general | solution.py:58
  194.9 5.4 %conditional.2 = ((f32[2,8,128]{2,1,0:T(8,128)S(1)}, f32[2,8,128]{2,1,0:T(8,128)S(1)}, f32[2,8,128,128]{3,2,1,0:T(8,128)S(1)})) conditional(s32[]{:T(128)} %convert_element_type.43, (f32[2,8,128]{2,1,0:T(8,128)S(1)}, f32[2,8,128]{2,1,0:T(8,128)S(1)}, f32[2,8,128,128]{3,2,1,0:T(8,128)S(1)}) %tuple.42, (pred[128,512]{0,1:T(8,128)(4,1)S(1)}, ...), branch_computations={%region_7.7_spmd, %region_8.10_spmd} | conditional | flops 551030784 | bytes 16057376 | solution.py:66
  197.7 2.6 %fusion.6 = f32[2,8,128,128]{3,2,1,0:T(8,128)S(1)} fusion(f32[2,512,128,8]{2,1,3,0:T(8,128)S(1)} %get-tuple-element.190, f32[2,8,128]{2,1,0:T(8,128)S(1)} %max.4, pred[128,512]{0,1:T(8,128)(4,1)S(1)} %get-tuple-element.115, f32[2,8,128,128]{3,2,1,0:T(8,128)S(1)} %get-tuple-element.120, f32[2,8,128]{2,1,0:T(8,128)S(1)} %get-tuple-element.186, ...), kind=kOutput, calls=%fused_computation.7 | convolution fusion | flops 274202624 | bytes 6636032 | tf_op jit(solution)/shard_map/while/body/eval_jaxpr/cond/branch_1_fun/hgqk,khd->hgqd/dot_general | solution.py:58
  201.9 5.4 %conditional.2 = ((f32[2,8,128]{2,1,0:T(8,128)S(1)}, f32[2,8,128]{2,1,0:T(8,128)S(1)}, f32[2,8,128,128]{3,2,1,0:T(8,128)S(1)})) conditional(s32[]{:T(128)} %convert_element_type.43, (f32[2,8,128]{2,1,0:T(8,128)S(1)}, f32[2,8,128]{2,1,0:T(8,128)S(1)}, f32[2,8,128,128]{3,2,1,0:T(8,128)S(1)}) %tuple.42, (pred[128,512]{0,1:T(8,128)(4,1)S(1)}, ...), branch_computations={%region_7.7_spmd, %region_8.10_spmd} | conditional | flops 551030784 | bytes 16057376 | solution.py:66
  204.6 2.6 %fusion.6 = f32[2,8,128,128]{3,2,1,0:T(8,128)S(1)} fusion(f32[2,512,128,8]{2,1,3,0:T(8,128)S(1)} %get-tuple-element.190, f32[2,8,128]{2,1,0:T(8,128)S(1)} %max.4, pred[128,512]{0,1:T(8,128)(4,1)S(1)} %get-tuple-element.115, f32[2,8,128,128]{3,2,1,0:T(8,128)S(1)} %get-tuple-element.120, f32[2,8,128]{2,1,0:T(8,128)S(1)} %get-tuple-element.186, ...), kind=kOutput, calls=%fused_computation.7 | convolution fusion | flops 274202624 | bytes 6636032 | tf_op jit(solution)/shard_map/while/body/eval_jaxpr/cond/branch_1_fun/hgqk,khd->hgqd/dot_general | solution.py:58
  208.8 5.4 %conditional.2 = ((f32[2,8,128]{2,1,0:T(8,128)S(1)}, f32[2,8,128]{2,1,0:T(8,128)S(1)}, f32[2,8,128,128]{3,2,1,0:T(8,128)S(1)})) conditional(s32[]{:T(128)} %convert_element_type.43, (f32[2,8,128]{2,1,0:T(8,128)S(1)}, f32[2,8,128]{2,1,0:T(8,128)S(1)}, f32[2,8,128,128]{3,2,1,0:T(8,128)S(1)}) %tuple.42, (pred[128,512]{0,1:T(8,128)(4,1)S(1)}, ...), branch_computations={%region_7.7_spmd, %region_8.10_spmd} | conditional | flops 551030784 | bytes 16057376 | solution.py:66
  211.6 2.7 %fusion.6 = f32[2,8,128,128]{3,2,1,0:T(8,128)S(1)} fusion(f32[2,512,128,8]{2,1,3,0:T(8,128)S(1)} %get-tuple-element.190, f32[2,8,128]{2,1,0:T(8,128)S(1)} %max.4, pred[128,512]{0,1:T(8,128)(4,1)S(1)} %get-tuple-element.115, f32[2,8,128,128]{3,2,1,0:T(8,128)S(1)} %get-tuple-element.120, f32[2,8,128]{2,1,0:T(8,128)S(1)} %get-tuple-element.186, ...), kind=kOutput, calls=%fused_computation.7 | convolution fusion | flops 274202624 | bytes 6636032 | tf_op jit(solution)/shard_map/while/body/eval_jaxpr/cond/branch_1_fun/hgqk,khd->hgqd/dot_general | solution.py:58
  215.8 5.4 %conditional.2 = ((f32[2,8,128]{2,1,0:T(8,128)S(1)}, f32[2,8,128]{2,1,0:T(8,128)S(1)}, f32[2,8,128,128]{3,2,1,0:T(8,128)S(1)})) conditional(s32[]{:T(128)} %convert_element_type.43, (f32[2,8,128]{2,1,0:T(8,128)S(1)}, f32[2,8,128]{2,1,0:T(8,128)S(1)}, f32[2,8,128,128]{3,2,1,0:T(8,128)S(1)}) %tuple.42, (pred[128,512]{0,1:T(8,128)(4,1)S(1)}, ...), branch_computations={%region_7.7_spmd, %region_8.10_spmd} | conditional | flops 551030784 | bytes 16057376 | solution.py:66
  215.8 1.7 fusion
  218.5 2.6 %fusion.6 = f32[2,8,128,128]{3,2,1,0:T(8,128)S(1)} fusion(f32[2,512,128,8]{2,1,3,0:T(8,128)S(1)} %get-tuple-element.190, f32[2,8,128]{2,1,0:T(8,128)S(1)} %max.4, pred[128,512]{0,1:T(8,128)(4,1)S(1)} %get-tuple-element.115, f32[2,8,128,128]{3,2,1,0:T(8,128)S(1)} %get-tuple-element.120, f32[2,8,128]{2,1,0:T(8,128)S(1)} %get-tuple-element.186, ...), kind=kOutput, calls=%fused_computation.7 | convolution fusion | flops 274202624 | bytes 6636032 | tf_op jit(solution)/shard_map/while/body/eval_jaxpr/cond/branch_1_fun/hgqk,khd->hgqd/dot_general | solution.py:58
  222.7 5.4 %conditional.2 = ((f32[2,8,128]{2,1,0:T(8,128)S(1)}, f32[2,8,128]{2,1,0:T(8,128)S(1)}, f32[2,8,128,128]{3,2,1,0:T(8,128)S(1)})) conditional(s32[]{:T(128)} %convert_element_type.43, (f32[2,8,128]{2,1,0:T(8,128)S(1)}, f32[2,8,128]{2,1,0:T(8,128)S(1)}, f32[2,8,128,128]{3,2,1,0:T(8,128)S(1)}) %tuple.42, (pred[128,512]{0,1:T(8,128)(4,1)S(1)}, ...), branch_computations={%region_7.7_spmd, %region_8.10_spmd} | conditional | flops 551030784 | bytes 16057376 | solution.py:66
  222.7 1.7 fusion
  225.4 2.6 %fusion.6 = f32[2,8,128,128]{3,2,1,0:T(8,128)S(1)} fusion(f32[2,512,128,8]{2,1,3,0:T(8,128)S(1)} %get-tuple-element.190, f32[2,8,128]{2,1,0:T(8,128)S(1)} %max.4, pred[128,512]{0,1:T(8,128)(4,1)S(1)} %get-tuple-element.115, f32[2,8,128,128]{3,2,1,0:T(8,128)S(1)} %get-tuple-element.120, f32[2,8,128]{2,1,0:T(8,128)S(1)} %get-tuple-element.186, ...), kind=kOutput, calls=%fused_computation.7 | convolution fusion | flops 274202624 | bytes 6636032 | tf_op jit(solution)/shard_map/while/body/eval_jaxpr/cond/branch_1_fun/hgqk,khd->hgqd/dot_general | solution.py:58
  228.6 8.2 %convolution_convert_fusion = bf16[128,4096]{1,0:T(8,128)(2,1)S(1)} fusion(bf16[128,2048]{0,1:T(8,128)(2,1)S(1)} %bitcast.44, bf16[2048,4096]{1,0:T(8,128)(2,1)} %param.15), kind=kOutput, calls=%fused_computation.23 | convolution fusion | flops 2148007936 | bytes 18350080 | tf_op jit(solution)/shard_map/dot_general | solution.py:138
  236.8 19.6 %all_to_all.5 = bf16[4,32,4096]{2,1,0:T(8,128)(2,1)S(1)} all-to-all(bf16[4,32,4096]{2,1,0:T(8,128)(2,1)S(1)} %bitcast.43), channel_id=1, replica_groups=mesh['cp'=64,'tp'=4] {'tp'}, dimensions={0} | all-to-all | bytes 2097152 | tf_op jit(solution)/shard_map/all_to_all | solution.py:29
  (122 shorter events, 46.5 us)
Async XLA Ops:
  6.5 85.9 %all-gather.2.cloned.1.call-start = ((), (), s32[]{:S(2)}) async-start(), calls=%async_computation.1 | async-start | bytes 8519680 | tf_op jit(solution)/shard_map/all_gather | solution.py:15
Sparse Core Ops, SparseCore 0:
  10.1 82.3 all-gather.1
where the time goes:
time: 268 us; the launch traced here: 264 us
  waiting for transfers between devices  79.8 us (30%)
  matrix products  73.2 us (27%)
  other arithmetic  34.1 us (13%)
  local copies, waits for them, and re-layouts  32.1 us (12%)
  blocking collectives  19.6 us (7%)
  between operations  13.5 us (5%)
  loops' own time  11.8 us (4%)
    all_gather x1, waiting for transfers between devices, in_one_piece(): lax.all_gather(both, axis, axis=dim, tiled=True)  79.8 us
    dot_general x15, matrix products, compute(): jnp.einsum('hgqk,khd->hgqd', weights.astype(jnp.bfloat16), value_rows, pr...  39.8 us
    dot_general x15, matrix products, compute(): jnp.einsum('qhgd,khd->hgqk', query_rows, key_rows, preferred_element_type...  25.3 us
    all_to_all x1, blocking collectives, sent_and_summed(): lax.all_to_all(cut_along(value, dim, length), axis, 0, 0, tiled=True)  19.6 us
    reduce_sum x15, other arithmetic, compute(): weight_sum = weight_sum * factor + jnp.sum(weights, axis=-1)  15 us
    reduce_or x16, other arithmetic, attend(): jnp.any(allowed)  13.4 us
    another operation x1, loops' own time, sweep_keys(): lax.scan(scan_step, online, (key_part.reshape(token_blocks, block_rows, h...  10.9 us
    while x4, local copies, waits for them, and re-layouts, sweep_keys(): lax.scan(scan_step, online, (key_part.reshape(token_blocks, block_rows, h...  10.9 us
  transfers between devices with their start and end apart: 1, of which 1 were waited for; matrix products, arithmetic and copies ran while one was open for 2% of the time, Pallas kernels for 0%

commit v1 on v0

v1 whole, which is shorter than its diff:
```python
import functools
import math

import jax
import jax.numpy as jnp
from jax import lax
from jax.experimental import pallas as pl
from jax.experimental.pallas import tpu as pltpu
from jax.sharding import PartitionSpec as P

BF16, F32 = jnp.bfloat16, jnp.float32
Z, X, TP = 8, 4, 4
ROWS, HEAD, HKV, GROUP = 128, 128, 2, 8
QL = GROUP * ROWS
WIN = 4096
TILE = 256
NCHUNK, COLS = 8, 512
ONES = 16
FAR = 1e30
SCALE = HEAD**-0.5 * math.log2(math.e)
DELTA = (0, -1, 1, 2)
MESH_ID = pl.DeviceIdType.MESH

ORDER = (
    ((0, 0), (1, 0), (0, -1), (1, -1), (0, 1), (1, 1), (1, -2), (0, -2), (1, 2), (0, 2), (1, -3), (1, 3), (0, -3), (1, 4), (0, 3), (0, 4)),
    ((1, 0), (0, 0), (1, -1), (0, -1), (1, 1), (0, 1), (1, -2), (1, 2), (0, -2), (0, 2), (1, -3), (1, 3), (0, -3), (0, 3), (1, 4), (0, 4)),
)


def events():
    both, k, v = "b", "k", "v"
    zero = [[] for _ in range(16)]
    zero[0] += [
        ((0, -1), (both,), [(k, "x+"), (both, "z+"), (both, "z-"), (both, "s")]),
        ((0, 1), (both,), [(v, "x-"), (both, "z+"), (both, "z-"), (both, "s")]),
    ]
    zero[1] += [((0, 2), (k, v), [(both, "z+"), (both, "z-"), (both, "s")])]
    for step in range(1, 4):
        for j in range(4):
            zero[4 * (step - 1) + j] += [
                ((-step, DELTA[j]), (both,), [(k if step == 3 else both, "z+"), (both, "s")]),
                ((step, DELTA[j]), (both,), [(v if step == 3 else both, "z-"), (both, "s")]),
            ]
    for j in range(4):
        zero[12 + j] += [((4, DELTA[j]), (k, v), [(both, "s")])]

    def along_z(step):
        if step == 4:
            return [((4, 0), (k, v), [(both, "x+"), (both, "x-"), (both, "s")])]
        return [
            ((-step, 0), (both,), [(k if step == 3 else both, "z+"), (both, "x+"), (both, "x-"), (both, "s")]),
            ((step, 0), (both,), [(v if step == 3 else both, "z-"), (both, "x+"), (both, "x-"), (both, "s")]),
        ]

    def near(dz):
        return [((dz, -1), (both,), [(k, "x+"), (both, "s")]), ((dz, 1), (both,), [(v, "x-"), (both, "s")])]

    def across(dz):
        return [((dz, 2), (k, v), [(both, "s")])]

    one = [
        near(0) + along_z(1),
        across(0),
        along_z(2) + near(-1),
        near(1) + across(-1),
        across(1) + along_z(3),
        near(-2),
        near(2) + across(-2),
        across(2) + along_z(4),
        near(-3),
        near(3) + across(-3),
        across(3) + near(4),
        across(4),
        [],
        [],
        [],
        [],
    ]
    return zero, one


def kernel(
    q_ref, k_ref, v_ref, doc_ref, ord_ref, w_ref, out_ref,
    buf, qin, vin, wbuf, qt, acc, mx, att, part, rin, sums, left_in, right_in, outv,
    recv, recv2, send, y_send, y_recv, local, w_sem,
):
    cp, tp = lax.axis_index("cp"), lax.axis_index("tp")
    core, x, z = lax.rem(cp, 2), lax.rem(cp // 2, X), cp // (2 * X)

    def block_of(kind, dz, dx):
        return kind * Z + lax.rem(z + dz + Z, Z), lax.rem(x + dx + X, X)

    def at(to):
        if to == "s":
            return (cp + 1 - 2 * core, tp)
        dz, dx = {"z+": (1, 0), "z-": (-1, 0), "x+": (0, 1), "x-": (0, -1)}[to]
        return ((lax.rem(z + dz + Z, Z) * X + lax.rem(x + dx + X, X)) * 2 + core, tp)

    def copy(group, col, piece, target, index):
        if piece == "b":
            ref, sem = buf.at[group, col], recv.at[group * X + col]
        elif piece == "k":
            ref, sem = buf.at[group, col, 0], recv.at[group * X + col]
        else:
            ref, sem = buf.at[group, col, 1], recv2.at[group * X + col]
        return pltpu.make_async_remote_copy(
            src_ref=ref, dst_ref=ref, send_sem=send.at[index], recv_sem=sem,
            device_id=target, device_id_type=MESH_ID,
        )

    my_group, my_col = core * Z + z, x
    neighbours = [at(to) for to in ("s", "z+", "z-", "x+", "x-")]
    up, down = (cp, lax.rem(tp + 1, TP)), (cp, lax.rem(tp + TP - 1, TP))
    neighbours += [up, down]

    loads = [
        pltpu.make_async_copy(v_ref, vin, local.at[0]),
        pltpu.make_async_copy(k_ref.at[:, 0:HEAD], buf.at[my_group, my_col, 0, 0], local.at[1]),
        pltpu.make_async_copy(k_ref.at[:, HEAD : 2 * HEAD], buf.at[my_group, my_col, 0, 1], local.at[2]),
        pltpu.make_async_copy(q_ref, qin, local.at[3]),
    ]
    for c in loads:
        c.start()
    weights = [
        pltpu.make_async_copy(
            w_ref.at[:, n * COLS : (n + 1) * COLS], wbuf.at[:, n * COLS : (n + 1) * COLS], w_sem.at[n]
        )
        for n in range(NCHUNK)
    ]
    barrier = pltpu.get_barrier_semaphore()
    for device in neighbours:
        pl.semaphore_signal(barrier, inc=1, device_id=device, device_id_type=MESH_ID)
    loads[0].wait()
    for h in range(HKV):
        vt = vin[:, h * HEAD : (h + 1) * HEAD].astype(F32).T.astype(BF16)
        buf[my_group, my_col, 1, h] = vt
    loads[1].wait()
    loads[2].wait()
    pl.semaphore_wait(barrier, len(neighbours))

    own_to = ("z+", "z-", "x+", "x-", "s")
    for i, to in enumerate(own_to):
        copy(my_group, my_col, "b", at(to), i).start()
    for c in weights:
        c.start()

    loads[3].wait()
    for h in range(HKV):
        for g in range(GROUP):
            i = h * GROUP + g
            scaled = (qin[:, i * HEAD : (i + 1) * HEAD].astype(F32) * SCALE).T
            high = scaled.astype(BF16)
            qt[h, 0:HEAD, g * ROWS : (g + 1) * ROWS] = high
            qt[h, HEAD : 2 * HEAD, g * ROWS : (g + 1) * ROWS] = (scaled - high.astype(F32)).astype(BF16)

    own_seq = ord_ref[cp]
    first_seq, end = jnp.int32(0), jnp.int32(0)
    for d in range(4):
        end = end + doc_ref[d]
        first_seq = jnp.where(end <= own_seq, end, first_seq)

    tiles = [(h, i) for h in range(HKV) for i in range(QL // TILE)]

    key_at = lax.broadcasted_iota(jnp.int32, (ROWS, TILE), 0)
    query_at = lax.rem(lax.broadcasted_iota(jnp.int32, (ROWS, TILE), 1), ROWS)
    seen = key_at <= query_at
    ones = jnp.ones((ONES, ROWS), BF16)
    for h, i in tiles:
        lanes = slice(i * TILE, (i + 1) * TILE)
        keys = buf[my_group, my_col, 0, h]
        s = jnp.dot(jnp.concatenate([keys, keys], axis=1), qt[h, :, lanes], preferred_element_type=F32)
        s = jnp.where(seen, s, -FAR)
        m = jnp.max(s, axis=0, keepdims=True)
        p = jnp.exp2(s - m).astype(BF16)
        values = jnp.concatenate([buf[my_group, my_col, 1, h], ones], axis=0)
        acc[h, :, lanes] = jnp.dot(values, p, preferred_element_type=F32)
        mx[h, :, lanes] = m

    plans = events()
    sends = ([(p, i) for i, p in enumerate("bbbbb")], [(p, i) for i, p in enumerate("bbbbb")])
    by_step = []
    for kind in range(2):
        index, steps = len(own_to), []
        for step in plans[kind]:
            now = []
            for where, waits, to in step:
                outs = []
                for piece, target in to:
                    outs.append((piece, target, index))
                    sends[kind].append((piece, index))
                    index += 1
                now.append((where, waits, outs))
            steps.append(now)
        by_step.append(steps)

    def communicate(t, kind):
        for (dz, dx), waits, outs in by_step[kind][t]:
            group, col = block_of(kind, dz, dx)
            for piece in waits:
                copy(group, col, piece, at("s"), 0).wait_recv()
            for piece, target, index in outs:
                copy(group, col, piece, at(target), index).start()

    def table(t, values):
        out = jnp.int32(values[0])
        for i in range(1, len(values)):
            out = jnp.where(t == i + 1, jnp.int32(values[i]), out)
        return out

    more_ones = jnp.ones((ONES, X * ROWS), BF16)

    def attend(group, biases):
        def scores(h, i):
            keys = buf[group, :, 0, h].reshape(X * ROWS, HEAD)
            return jnp.dot(
                jnp.concatenate([keys, keys], axis=1),
                qt[h, :, i * TILE : (i + 1) * TILE],
                preferred_element_type=F32,
            )

        coming = scores(*tiles[0])
        for n, (h, i) in enumerate(tiles):
            s = coming
            if n + 1 < len(tiles):
                coming = scores(*tiles[n + 1])
            lanes = slice(i * TILE, (i + 1) * TILE)
            blocks = [s[j * ROWS : (j + 1) * ROWS] for j in range(X)]
            old = mx[h, :, lanes]
            m = old
            for j in range(X):
                m = jnp.maximum(m, jnp.max(blocks[j], axis=0, keepdims=True) - biases[j])
            factor = jnp.exp2(old - m)
            p = jnp.concatenate([jnp.exp2(blocks[j] - (m + biases[j])).astype(BF16) for j in range(X)], axis=0)
            values = jnp.concatenate([buf[group, j, 1, h] for j in range(X)], axis=1)
            values = jnp.concatenate([values, more_ones], axis=0)
            acc[h, :, lanes] = acc[h, :, lanes] * factor + jnp.dot(values, p, preferred_element_type=F32)
            mx[h, :, lanes] = m

    for kind in range(2):

        @pl.when(core == kind)
        def _(kind=kind):
            communicate(0, kind)

    def step(t, carry):
        for i in range(1, 16):
            for kind in range(2):
                if by_step[kind][i]:

                    @pl.when((t == i) & (core == kind))
                    def _(i=i, kind=kind):
                        communicate(i, kind)

        kind = jnp.where(core == 0, table(t, [g for g, _ in ORDER[0]]), table(t, [g for g, _ in ORDER[1]]))
        away = jnp.where(core == 0, table(t, [d for _, d in ORDER[0]]), table(t, [d for _, d in ORDER[1]]))
        zz = lax.rem(z + away + Z, Z)
        group = kind * Z + zz

        @pl.when(kind != core)
        def _():
            for j in range(X):
                copy(group, j, "b", at("s"), 0).wait_recv()

        biases = []
        for j in range(X):
            seq = ord_ref[(zz * X + j) * 2 + kind]
            biases.append(jnp.where((seq >= first_seq) & (seq < own_seq), 0.0, FAR))
        attend(group, biases)
        return carry

    lax.fori_loop(1, 17, step, 0)

    for h in range(HKV):
        for g in range(GROUP):
            lanes = slice(g * ROWS, (g + 1) * ROWS)
            a = acc[h, 0:HEAD, lanes] / acc[h, HEAD : HEAD + 1, lanes]
            i = h * GROUP + g
            att[:, i * HEAD : (i + 1) * HEAD] = a.T.astype(BF16)

    own, above, below, over = tp, up[1], down[1], lax.rem(tp + 2, TP)
    half = NCHUNK // 2
    chunks = [n // 2 + (n % 2) * half for n in range(NCHUNK)]

    def y_copy(src, dst, index, target):
        return pltpu.make_async_remote_copy(
            src_ref=src, dst_ref=dst, send_sem=y_send.at[index], recv_sem=y_recv.at[index],
            device_id=target, device_id_type=MESH_ID,
        )

    def relay(n):
        return y_copy(part.at[n, over], rin.at[n], n, up if n < half else down)

    def direct(n):
        if n < half:
            return y_copy(part.at[n, below], right_in.at[n], NCHUNK + n, down)
        return y_copy(part.at[n, above], left_in.at[n], NCHUNK + n, up)

    def summed(n):
        if n < half:
            return y_copy(sums.at[n], left_in.at[n], 2 * NCHUNK + n, up)
        return y_copy(sums.at[n], right_in.at[n], 2 * NCHUNK + n, down)

    attended = att[...]
    ready = None
    for n in chunks:
        weights[n].wait()
        piece = jnp.dot(attended, wbuf[:, n * COLS : (n + 1) * COLS], preferred_element_type=F32)
        part[n] = piece.astype(BF16).reshape(TP, ROWS // TP, COLS)
        if ready is not None:
            relay(ready).start()
            direct(ready).start()
        ready = n
    relay(ready).start()
    direct(ready).start()
    ready = None
    for n in chunks:
        relay(n).wait_recv()
        onward = above if n < half else below
        sums[n] = (rin[n].astype(F32) + part[n, onward].astype(F32)).astype(BF16)
        if ready is not None:
            summed(ready).start()
        ready = n
    summed(ready).start()
    outs = []
    for n in chunks:
        direct(n).wait_recv()
        summed(n).wait_recv()
        total = part[n, own].astype(F32) + left_in[n].astype(F32) + right_in[n].astype(F32)
        outv[:, n * COLS : (n + 1) * COLS] = total.astype(BF16)
        outs.append(
            pltpu.make_async_copy(
                outv.at[:, n * COLS : (n + 1) * COLS], out_ref.at[:, n * COLS : (n + 1) * COLS], w_sem.at[n]
            )
        )
        outs[-1].start()

    for n in range(NCHUNK):
        relay(n).wait_send()
        direct(n).wait_send()
        summed(n).wait_send()
    for kind in range(2):

        @pl.when(core == kind)
        def _(kind=kind):
            for piece, index in sends[kind]:
                copy(my_group, my_col, piece, at("s"), index).wait_send()

    for c in outs:
        c.wait()


def local(queries, keys, values, doc_blocks, block_order, out_weight):
    any_, smem = pl.BlockSpec(memory_space=pl.ANY), pl.BlockSpec(memory_space=pltpu.SMEM)
    rows = ROWS // TP
    return pl.pallas_call(
        kernel,
        out_shape=jax.ShapeDtypeStruct((rows, WIN), BF16),
        in_specs=[any_, any_, any_, smem, smem, any_],
        out_specs=any_,
        scratch_shapes=[
            pltpu.VMEM((2 * Z, X, 2, HKV, ROWS, HEAD), BF16),
            pltpu.VMEM((ROWS, HKV * GROUP * HEAD), BF16),
            pltpu.VMEM((ROWS, HKV * HEAD), BF16),
            pltpu.VMEM((HKV * GROUP * HEAD, WIN), BF16),
            pltpu.VMEM((HKV, 2 * HEAD, QL), BF16),
            pltpu.VMEM((HKV, HEAD + ONES, QL), F32),
            pltpu.VMEM((HKV, 1, QL), F32),
            pltpu.VMEM((ROWS, HKV * GROUP * HEAD), BF16),
            pltpu.VMEM((NCHUNK, TP, rows, COLS), BF16),
            pltpu.VMEM((NCHUNK, rows, COLS), BF16),
            pltpu.VMEM((NCHUNK, rows, COLS), BF16),
            pltpu.VMEM((NCHUNK, rows, COLS), BF16),
            pltpu.VMEM((NCHUNK, rows, COLS), BF16),
            pltpu.VMEM((rows, WIN), BF16),
            pltpu.SemaphoreType.DMA((2 * Z * X,)),
            pltpu.SemaphoreType.DMA((2 * Z * X,)),
            pltpu.SemaphoreType.DMA((96,)),
            pltpu.SemaphoreType.DMA((3 * NCHUNK,)),
            pltpu.SemaphoreType.DMA((3 * NCHUNK,)),
            pltpu.SemaphoreType.DMA((4,)),
            pltpu.SemaphoreType.DMA((NCHUNK,)),
        ],
        compiler_params=pltpu.CompilerParams(
            collective_id=0, has_side_effects=True, vmem_limit_bytes=60 * 1024 * 1024
        ),
        name="attention",
    )(queries, keys, values, doc_blocks, block_order, out_weight)


def solution(mesh):
    placed = (P("cp", "tp"), P("cp", "tp"), P("cp", "tp"), P(), P(), P("tp", None))
    return jax.shard_map(
        local, mesh=mesh, in_specs=placed, out_specs=P(("cp", "tp"), None), check_vma=False
    )
```

time: 268 us -> 76.6 us (0.29)
  the two profiles are of different devices: /device:TPU:68 before, /device:TPU:1 now
where the time goes in v1:
time: 76.6 us; the launch traced here: 76.5 us
  Pallas kernels  74.8 us (98%)
  local copies, waits for them, and re-layouts  1.67 us (2%)
    pallas_call x1, Pallas kernels, local(): pl.pallas_call(kernel, out_shape=jax.ShapeDtypeStruct((rows, WIN), BF16),...  74.8 us
    unnamed x1, local copies, waits for them, and re-layouts  1.67 us

profile of v1, /device:TPU:1, one launch (start us, length us, event | category | flops | bytes accessed | tf_op | source)
XLA Modules:
  0.0 76.5 jit_solution(16967012323521601969)
XLA Ops:
  0.0 74.8 %attention.1 = bf16[32,4096]{1,0:T(8,128)(2,1)} custom-call(bf16[128,2048]{1,0:T(8,128)(2,1)} %q_ref.1, bf16[128,256]{1,0:T(8,128)(2,1)} %k_ref.1, bf16[128,256]{1,0:T(8,128)(2,1)} %v_ref.1, s32[4]{0:T(128)} %doc_ref.1, s32[64]{0:T(128)} %ord_ref.1, bf16[2048,4096]{1,0:T(8,128)(2,1)} %w_ref.1), custom_call_target="tpu_custom_call" | custom-call | tf_op jit(solution)/shard_map/attention/pallas_call | solution.py:355
  74.8 1.7 %copy.8 = bf16[32,4096]{1,0:T(8,128)(2,1)} copy(bf16[32,4096]{1,0:T(8,128)(2,1)} %attention.1) | data formatting | bytes 524288

commit v2 on v1

--- a/solution.py
+++ b/solution.py
@@ -130,13 +130,14 @@
     barrier = pltpu.get_barrier_semaphore()
     for device in neighbours:
         pl.semaphore_signal(barrier, inc=1, device_id=device, device_id_type=MESH_ID)
-    loads[0].wait()
-    for h in range(HKV):
-        vt = vin[:, h * HEAD : (h + 1) * HEAD].astype(F32).T.astype(BF16)
-        buf[my_group, my_col, 1, h] = vt
-    loads[1].wait()
-    loads[2].wait()
-    pl.semaphore_wait(barrier, len(neighbours))
+    with jax.named_scope("entry"):
+        loads[0].wait()
+        for h in range(HKV):
+            vt = vin[:, h * HEAD : (h + 1) * HEAD].astype(F32).T.astype(BF16)
+            buf[my_group, my_col, 1, h] = vt
+        loads[1].wait()
+        loads[2].wait()
+        pl.semaphore_wait(barrier, len(neighbours))
 
     own_to = ("z+", "z-", "x+", "x-", "s")
     for i, to in enumerate(own_to):
@@ -144,14 +145,15 @@
     for c in weights:
         c.start()
 
-    loads[3].wait()
-    for h in range(HKV):
-        for g in range(GROUP):
-            i = h * GROUP + g
-            scaled = (qin[:, i * HEAD : (i + 1) * HEAD].astype(F32) * SCALE).T
-            high = scaled.astype(BF16)
-            qt[h, 0:HEAD, g * ROWS : (g + 1) * ROWS] = high
-            qt[h, HEAD : 2 * HEAD, g * ROWS : (g + 1) * ROWS] = (scaled - high.astype(F32)).astype(BF16)
+    with jax.named_scope("queries"):
+        loads[3].wait()
+        for h in range(HKV):
+            for g in range(GROUP):
+                i = h * GROUP + g
+                scaled = (qin[:, i * HEAD : (i + 1) * HEAD].astype(F32) * SCALE).T
+                high = scaled.astype(BF16)
+                qt[h, 0:HEAD, g * ROWS : (g + 1) * ROWS] = high
+                qt[h, HEAD : 2 * HEAD, g * ROWS : (g + 1) * ROWS] = (scaled - high.astype(F32)).astype(BF16)
 
     own_seq = ord_ref[cp]
     first_seq, end = jnp.int32(0), jnp.int32(0)
@@ -165,16 +167,17 @@
     query_at = lax.rem(lax.broadcasted_iota(jnp.int32, (ROWS, TILE), 1), ROWS)
     seen = key_at <= query_at
     ones = jnp.ones((ONES, ROWS), BF16)
-    for h, i in tiles:
-        lanes = slice(i * TILE, (i + 1) * TILE)
-        keys = buf[my_group, my_col, 0, h]
-        s = jnp.dot(jnp.concatenate([keys, keys], axis=1), qt[h, :, lanes], preferred_element_type=F32)
-        s = jnp.where(seen, s, -FAR)
-        m = jnp.max(s, axis=0, keepdims=True)
-        p = jnp.exp2(s - m).astype(BF16)
-        values = jnp.concatenate([buf[my_group, my_col, 1, h], ones], axis=0)
-        acc[h, :, lanes] = jnp.dot(values, p, preferred_element_type=F32)
-        mx[h, :, lanes] = m
+    with jax.named_scope("own"):
+        for h, i in tiles:
+            lanes = slice(i * TILE, (i + 1) * TILE)
+            keys = buf[my_group, my_col, 0, h]
+            s = jnp.dot(jnp.concatenate([keys, keys], axis=1), qt[h, :, lanes], preferred_element_type=F32)
+            s = jnp.where(seen, s, -FAR)
+            m = jnp.max(s, axis=0, keepdims=True)
+            p = jnp.exp2(s - m).astype(BF16)
+            values = jnp.concatenate([buf[my_group, my_col, 1, h], ones], axis=0)
+            acc[h, :, lanes] = jnp.dot(values, p, preferred_element_type=F32)
+            mx[h, :, lanes] = m
 
     plans = events()
     sends = ([(p, i) for i, p in enumerate("bbbbb")], [(p, i) for i, p in enumerate("bbbbb")])
@@ -200,12 +203,6 @@
                 copy(group, col, piece, at("s"), 0).wait_recv()
             for piece, target, index in outs:
                 copy(group, col, piece, at(target), index).start()
-
-    def table(t, values):
-        out = jnp.int32(values[0])
-        for i in range(1, len(values)):
-            out = jnp.where(t == i + 1, jnp.int32(values[i]), out)
-        return out
 
     more_ones = jnp.ones((ONES, X * ROWS), BF16)
 
@@ -240,42 +237,49 @@
 
         @pl.when(core == kind)
         def _(kind=kind):
-            communicate(0, kind)
+            with jax.named_scope("step0"):
+                communicate(0, kind)
 
     def step(t, carry):
-        for i in range(1, 16):
-            for kind in range(2):
-                if by_step[kind][i]:
-
-                    @pl.when((t == i) & (core == kind))
-                    def _(i=i, kind=kind):
-                        communicate(i, kind)
-
-        kind = jnp.where(core == 0, table(t, [g for g, _ in ORDER[0]]), table(t, [g for g, _ in ORDER[1]]))
-        away = jnp.where(core == 0, table(t, [d for _, d in ORDER[0]]), table(t, [d for _, d in ORDER[1]]))
+        def dispatch(kind, low, high):
+            if high - low > 1:
+                middle = (low + high) // 2
+                return lax.cond(
+                    t < middle, lambda: dispatch(kind, low, middle), lambda: dispatch(kind, middle, high)
+                )
+            if low < 16 and by_step[kind][low]:
+                with jax.named_scope(f"step{low}"):
+                    communicate(low, kind)
+            of, away = ORDER[kind][low - 1]
+            return jnp.int32(of), jnp.int32(away)
+
+        kind, away = lax.cond(core == 0, lambda: dispatch(0, 1, 17), lambda: dispatch(1, 1, 17))
         zz = lax.rem(z + away + Z, Z)
         group = kind * Z + zz
 
         @pl.when(kind != core)
         def _():
-            for j in range(X):
-                copy(group, j, "b", at("s"), 0).wait_recv()
+            with jax.named_scope("sibling"):
+                for j in range(X):
+                    copy(group, j, "b", at("s"), 0).wait_recv()
 
         biases = []
         for j in range(X):
             seq = ord_ref[(zz * X + j) * 2 + kind]
             biases.append(jnp.where((seq >= first_seq) & (seq < own_seq), 0.0, FAR))
-        attend(group, biases)
+        with jax.named_scope("attend"):
+            attend(group, biases)
         return carry
 
     lax.fori_loop(1, 17, step, 0)
 
-    for h in range(HKV):
-        for g in range(GROUP):
-            lanes = slice(g * ROWS, (g + 1) * ROWS)
-            a = acc[h, 0:HEAD, lanes] / acc[h, HEAD : HEAD + 1, lanes]
-            i = h * GROUP + g
-            att[:, i * HEAD : (i + 1) * HEAD] = a.T.astype(BF16)
+    with jax.named_scope("attended"):
+        for h in range(HKV):
+            for g in range(GROUP):
+                lanes = slice(g * ROWS, (g + 1) * ROWS)
+                a = acc[h, 0:HEAD, lanes] / acc[h, HEAD : HEAD + 1, lanes]
+                i = h * GROUP + g
+                att[:, i * HEAD : (i + 1) * HEAD] = a.T.astype(BF16)
 
     own, above, below, over = tp, up[1], down[1], lax.rem(tp + 2, TP)
     half = NCHUNK // 2
@@ -300,39 +304,40 @@
             return y_copy(sums.at[n], left_in.at[n], 2 * NCHUNK + n, up)
         return y_copy(sums.at[n], right_in.at[n], 2 * NCHUNK + n, down)
 
-    attended = att[...]
-    ready = None
-    for n in chunks:
-        weights[n].wait()
-        piece = jnp.dot(attended, wbuf[:, n * COLS : (n + 1) * COLS], preferred_element_type=F32)
-        part[n] = piece.astype(BF16).reshape(TP, ROWS // TP, COLS)
-        if ready is not None:
-            relay(ready).start()
-            direct(ready).start()
-        ready = n
-    relay(ready).start()
-    direct(ready).start()
-    ready = None
-    for n in chunks:
-        relay(n).wait_recv()
-        onward = above if n < half else below
-        sums[n] = (rin[n].astype(F32) + part[n, onward].astype(F32)).astype(BF16)
-        if ready is not None:
-            summed(ready).start()
-        ready = n
-    summed(ready).start()
-    outs = []
-    for n in chunks:
-        direct(n).wait_recv()
-        summed(n).wait_recv()
-        total = part[n, own].astype(F32) + left_in[n].astype(F32) + right_in[n].astype(F32)
-        outv[:, n * COLS : (n + 1) * COLS] = total.astype(BF16)
-        outs.append(
-            pltpu.make_async_copy(
-                outv.at[:, n * COLS : (n + 1) * COLS], out_ref.at[:, n * COLS : (n + 1) * COLS], w_sem.at[n]
+    with jax.named_scope("project"):
+        attended = att[...]
+        ready = None
+        for n in chunks:
+            weights[n].wait()
+            piece = jnp.dot(attended, wbuf[:, n * COLS : (n + 1) * COLS], preferred_element_type=F32)
+            part[n] = piece.astype(BF16).reshape(TP, ROWS // TP, COLS)
+            if ready is not None:
+                relay(ready).start()
+                direct(ready).start()
+            ready = n
+        relay(ready).start()
+        direct(ready).start()
+        ready = None
+        for n in chunks:
+            relay(n).wait_recv()
+            onward = above if n < half else below
+            sums[n] = (rin[n].astype(F32) + part[n, onward].astype(F32)).astype(BF16)
+            if ready is not None:
+                summed(ready).start()
+            ready = n
+        summed(ready).start()
+        outs = []
+        for n in chunks:
+            direct(n).wait_recv()
+            summed(n).wait_recv()
+            total = part[n, own].astype(F32) + left_in[n].astype(F32) + right_in[n].astype(F32)
+            outv[:, n * COLS : (n + 1) * COLS] = total.astype(BF16)
+            outs.append(
+                pltpu.make_async_copy(
+                    outv.at[:, n * COLS : (n + 1) * COLS], out_ref.at[:, n * COLS : (n + 1) * COLS], w_sem.at[n]
+                )
             )
-        )
-        outs[-1].start()
+            outs[-1].start()
 
     for n in range(NCHUNK):
         relay(n).wait_send()

time: 76.6 us -> 68.6 us (0.90)
  Pallas kernels: 74.8 us -> 66.8 us
    pallas_call x1, Pallas kernels: 74.8 us -> 66.8 us  [local(): pl.pallas_call(kernel, out_shape=jax.ShapeDtypeStruct((rows, WIN), BF16),...]
where the time goes in v2:
time: 68.6 us; the launch traced here: 68.5 us
  Pallas kernels  66.8 us (97%)
  local copies, waits for them, and re-layouts  1.67 us (2%)
    pallas_call x1, Pallas kernels, local(): pl.pallas_call(kernel, out_shape=jax.ShapeDtypeStruct((rows, WIN), BF16),...  66.8 us
    unnamed x1, local copies, waits for them, and re-layouts  1.67 us

profile of v2, /device:TPU:1, one launch (start us, length us, event | category | flops | bytes accessed | tf_op | source)
XLA Modules:
  0.0 68.5 jit_solution(14974216844262212203)
XLA Ops:
  0.0 66.8 %attention.1 = bf16[32,4096]{1,0:T(8,128)(2,1)} custom-call(bf16[128,2048]{1,0:T(8,128)(2,1)} %q_ref.1, bf16[128,256]{1,0:T(8,128)(2,1)} %k_ref.1, bf16[128,256]{1,0:T(8,128)(2,1)} %v_ref.1, s32[4]{0:T(128)} %doc_ref.1, s32[64]{0:T(128)} %ord_ref.1, bf16[2048,4096]{1,0:T(8,128)(2,1)} %w_ref.1), custom_call_target="tpu_custom_call" | custom-call | tf_op jit(solution)/shard_map/attention/pallas_call | solution.py:360
  66.8 1.7 %copy.8 = bf16[32,4096]{1,0:T(8,128)(2,1)} copy(bf16[32,4096]{1,0:T(8,128)(2,1)} %attention.1) | data formatting | bytes 524288

commit v3 on v2

v3 whole, which is shorter than its diff:
```python
import functools
import math

import jax
import jax.numpy as jnp
from jax import lax
from jax.experimental import pallas as pl
from jax.experimental.pallas import tpu as pltpu
from jax.sharding import PartitionSpec as P

BF16, F32 = jnp.bfloat16, jnp.float32
Z, X, TP = 8, 4, 4
ROWS, HEAD, HKV, GROUP = 128, 128, 2, 8
QL = GROUP * ROWS
WIN = 4096
TILE = 256
NCHUNK, COLS = 8, 512
ONES = 16
FAR = 1e30
SCALE = HEAD**-0.5 * math.log2(math.e)
MESH_ID = pl.DeviceIdType.MESH

PLAN = (
    (
        (((-1, 0), (1, 0), (0, -1), (0, 1)), ((1, 0, 0), (0, -1, 0), (0, 1, 0), (0, 0, 0))),
        ((), ((0, 0, -1), (0, 0, 1), (1, -1, 0), (1, 1, 0))),
        (((0, 2), (-2, 0), (2, 0)), ((1, 0, -1), (1, 0, 1), (0, 0, 2), (0, -2, 0))),
        (((-1, -1), (1, -1)), ((0, 2, 0), (1, -1, -1), (1, -1, 1), (0, -1, -1))),
        (((-1, 1), (1, 1)), ((0, 1, -1), (1, -2, 0), (1, 2, 0), (1, 1, -1))),
        ((), ((1, 1, 1), (0, -1, 1), (0, 1, 1), (1, 0, 2))),
        (((-1, 2), (1, 2)), ((1, -1, 2), (1, -2, -1), (1, -2, 1), (0, -1, 2))),
        (((-3, 0), (3, 0)), ((0, 1, 2), (1, -3, 0), (1, 3, 0), (1, 2, -1))),
        (((-2, -1), (2, -1)), ((1, 2, 1), (0, -3, 0), (0, 3, 0), (1, 1, 2))),
        (((-2, 1), (2, 1)), ((1, -2, 2), (0, -2, -1), (0, 2, -1), (0, -2, 1))),
        (((-2, 2), (2, 2)), ((0, 2, 1), (1, 4, 0), (1, -3, -1), (1, -3, 1))),
        (((4, 0),), ((0, -2, 2), (0, 2, 2), (1, 3, -1), (1, 3, 1))),
        (((-3, -1), (3, -1)), ((1, 2, 2), (0, 4, 0), (0, -3, -1), (0, 3, -1))),
        (((-3, 1), (3, 1)), ((1, 4, -1), (1, 4, 1), (1, -3, 2), (0, -3, 1))),
        (((-3, 2), (3, 2), (4, -1), (4, 1)), ((0, 3, 1), (1, 3, 2), (0, -3, 2), (0, 3, 2))),
        (((4, 2),), ((0, 4, -1), (0, 4, 1), (1, 4, 2), (0, 4, 2))),
    ),
    (
        (((-1, 0), (1, 0), (0, -1), (0, 1)), ((0, 0, 0), (1, -1, 0), (1, 1, 0), (1, 0, 0))),
        ((), ((1, 0, -1), (1, 0, 1), (0, -1, 0), (0, 1, 0))),
        (((-1, -1), (-1, 1)), ((0, 0, -1), (0, 0, 1), (1, -1, -1), (1, -1, 1))),
        (((-2, 0), (2, 0), (1, -1), (1, 1)), ((0, 0, 2), (1, -2, 0), (1, 2, 0), (1, 1, -1))),
        (((0, 2), (-1, 2)), ((1, 1, 1), (0, -2, 0), (0, 2, 0), (1, 0, 2))),
        (((-2, -1), (-2, 1)), ((1, -1, 2), (0, -1, -1), (0, 1, -1), (1, -2, -1))),
        (((-3, 0), (3, 0), (2, -1), (2, 1)), ((1, -2, 1), (0, -1, 1), (0, 1, 1), (1, -3, 0))),
        (((1, 2), (-2, 2)), ((1, 3, 0), (1, 2, -1), (1, 2, 1), (1, 1, 2))),
        ((), ((1, -2, 2), (0, -1, 2), (0, 1, 2), (0, -3, 0))),
        (((4, 0), (-3, -1), (-3, 1), (3, -1), (3, 1)), ((0, 3, 0), (0, -2, -1), (1, 4, 0), (1, -3, -1))),
        (((2, 2),), ((1, -3, 1), (1, 3, -1), (1, 3, 1), (0, 2, -1))),
        ((), ((0, -2, 1), (1, 2, 2), (0, 2, 1), (0, -2, 2))),
        (((4, -1), (4, 1), (-3, 2)), ((0, 2, 2), (0, 4, 0), (1, 4, -1), (1, 4, 1))),
        (((3, 2),), ((1, -3, 2), (0, -3, -1), (1, 3, 2), (0, 3, -1))),
        (((4, 2),), ((0, -3, 1), (0, 3, 1), (1, 4, 2), (0, -3, 2))),
        ((), ((0, 3, 2), (0, 4, -1), (0, 4, 1), (0, 4, 2))),
    ),
)


def routes(kind, dz, dx):
    z_way, z_piece = ("z+", "k") if dz < 0 else ("z-", "v")
    z_out = [("b" if abs(dz) < 3 else z_piece, z_way)] if 0 < abs(dz) < 4 else []
    turn = [("k", "x+")] if dx == -1 else [("v", "x-")] if dx == 1 else []
    wide = [("b", "x+"), ("b", "x-")]
    if dz == 0 and dx == 0:
        out = [("b", "z+"), ("b", "z-")] + wide
    elif kind == 0 and dz == 0:
        out = [("b", "z+"), ("b", "z-")] + turn
    elif kind == 0 and dz == 4:
        out = wide if dx == 0 else turn
    elif kind == 0:
        out = z_out if abs(dz) < 3 or dx == 0 else []
    else:
        out = z_out + wide if dx == 0 else turn
    return out + [("b", "s")]


def pieces(kind, dz, dx):
    if kind == 0:
        return "kv" if dx == 2 and dz in (0, 4) or (dz, dx) == (4, 0) else "b"
    return "kv" if dx == 2 or (dz, dx) == (4, 0) else "b"


def slot_of(kind, dz, dx):
    return (kind * Z + dz % Z) * X + dx % X


def second_sem(kind, dz, dx):
    if kind == 0:
        return {(0, 2): 0, (4, 0): 1, (4, 2): 2}[dz, dx]
    return 0 if dx == 0 else 1 + dz % Z


def kernel(
    q_ref, k_ref, v_ref, doc_ref, ord_ref, w_ref, out_ref,
    buf, qin, vin, wbuf, qt, acc, mx, att, part, rin, sums, left_in, right_in, outv,
    recv, recv2, send, y_send, y_recv, local, w_sem,
):
    cp, tp = lax.axis_index("cp"), lax.axis_index("tp")
    core, x, z = lax.rem(cp, 2), lax.rem(cp // 2, X), cp // (2 * X)

    def at(to):
        if to == "s":
            return (cp + 1 - 2 * core, tp)
        dz, dx = {"z+": (1, 0), "z-": (-1, 0), "x+": (0, 1), "x-": (0, -1)}[to]
        return ((lax.rem(z + dz + Z, Z) * X + lax.rem(x + dx + X, X)) * 2 + core, tp)

    def copy(kind, dz, dx, piece, to):
        mz, mx_ = {"s": (0, 0), "z+": (-1, 0), "z-": (1, 0), "x+": (0, -1), "x-": (0, 1)}[to]
        there = (kind, (dz + mz + 3) % Z - 3, (dx + mx_ + 1) % X - 1)
        here, dest = slot_of(kind, dz, dx), slot_of(*there)
        src, dst, sem = buf.at[here], buf.at[dest], recv.at[dest]
        if piece == "k":
            src, dst = buf.at[here, 0], buf.at[dest, 0]
        elif piece == "v":
            src, dst, sem = buf.at[here, 1], buf.at[dest, 1], recv2.at[second_sem(*there)]
        return pltpu.make_async_remote_copy(
            src_ref=src, dst_ref=dst, send_sem=send, recv_sem=sem, device_id=at(to), device_id_type=MESH_ID
        )

    def arrived(kind, dz, dx, how):
        slot = slot_of(kind, dz, dx)
        for piece in how:
            ref, sem = buf.at[slot], recv.at[slot]
            if piece == "k":
                ref = buf.at[slot, 0]
            elif piece == "v":
                ref, sem = buf.at[slot, 1], recv2.at[second_sem(kind, dz, dx)]
            pltpu.make_async_remote_copy(
                src_ref=ref, dst_ref=ref, send_sem=send, recv_sem=sem, device_id=at("s"), device_id_type=MESH_ID
            ).wait_recv()

    my_slot = core * (Z * X)
    neighbours = [at(to) for to in ("s", "z+", "z-", "x+", "x-")]
    up, down = (cp, lax.rem(tp + 1, TP)), (cp, lax.rem(tp + TP - 1, TP))
    neighbours += [up, down]

    loads = [
        pltpu.make_async_copy(v_ref, vin, local.at[0]),
        pltpu.make_async_copy(k_ref.at[:, 0:HEAD], buf.at[my_slot, 0, 0], local.at[1]),
        pltpu.make_async_copy(k_ref.at[:, HEAD : 2 * HEAD], buf.at[my_slot, 0, 1], local.at[2]),
        pltpu.make_async_copy(q_ref, qin, local.at[3]),
    ]
    for c in loads:
        c.start()
    weights = [
        pltpu.make_async_copy(
            w_ref.at[:, n * COLS : (n + 1) * COLS], wbuf.at[:, n * COLS : (n + 1) * COLS], w_sem.at[n]
        )
        for n in range(NCHUNK)
    ]
    barrier = pltpu.get_barrier_semaphore()
    for device in neighbours:
        pl.semaphore_signal(barrier, inc=1, device_id=device, device_id_type=MESH_ID)
    with jax.named_scope("entry"):
        loads[0].wait()
        for h in range(HKV):
            vt = vin[:, h * HEAD : (h + 1) * HEAD].astype(F32).T.astype(BF16)
            buf[my_slot, 1, h] = vt
        loads[1].wait()
        loads[2].wait()
        pl.semaphore_wait(barrier, len(neighbours))

    for kind in range(2):

        @pl.when(core == kind)
        def _(kind=kind):
            for piece, to in routes(kind, 0, 0):
                copy(kind, 0, 0, piece, to).start()

    for c in weights:
        c.start()

    with jax.named_scope("queries"):
        loads[3].wait()
        for h in range(HKV):
            for g in range(GROUP):
                i = h * GROUP + g
                scaled = (qin[:, i * HEAD : (i + 1) * HEAD].astype(F32) * SCALE).T
                high = scaled.astype(BF16)
                qt[h, 0:HEAD, g * ROWS : (g + 1) * ROWS] = high
                qt[h, HEAD : 2 * HEAD, g * ROWS : (g + 1) * ROWS] = (scaled - high.astype(F32)).astype(BF16)

    own_seq = ord_ref[cp]
    first_seq, end = jnp.int32(0), jnp.int32(0)
    for d in range(4):
        end = end + doc_ref[d]
        first_seq = jnp.where(end <= own_seq, end, first_seq)

    tiles = [(h, i) for h in range(HKV) for i in range(QL // TILE)]

    key_at = lax.broadcasted_iota(jnp.int32, (ROWS, TILE), 0)
    query_at = lax.rem(lax.broadcasted_iota(jnp.int32, (ROWS, TILE), 1), ROWS)
    seen = key_at <= query_at
    ones = jnp.ones((ONES, ROWS), BF16)
    with jax.named_scope("own"):
        for h, i in tiles:
            lanes = slice(i * TILE, (i + 1) * TILE)
            keys = buf[my_slot, 0, h]
            s = jnp.dot(jnp.concatenate([keys, keys], axis=1), qt[h, :, lanes], preferred_element_type=F32)
            s = jnp.where(seen, s, -FAR)
            m = jnp.max(s, axis=0, keepdims=True)
            p = jnp.exp2(s - m).astype(BF16)
            values = jnp.concatenate([buf[my_slot, 1, h], ones], axis=0)
            acc[h, :, lanes] = jnp.dot(values, p, preferred_element_type=F32)
            mx[h, :, lanes] = m

    more_ones = jnp.ones((ONES, X * ROWS), BF16)

    def attend(slots, biases):
        def scores(h, i):
            keys = jnp.concatenate([buf[slot, 0, h] for slot in slots], axis=0)
            return jnp.dot(
                jnp.concatenate([keys, keys], axis=1),
                qt[h, :, i * TILE : (i + 1) * TILE],
                preferred_element_type=F32,
            )

        coming = scores(*tiles[0])
        for n, (h, i) in enumerate(tiles):
            s = coming
            if n + 1 < len(tiles):
                coming = scores(*tiles[n + 1])
            lanes = slice(i * TILE, (i + 1) * TILE)
            blocks = [s[j * ROWS : (j + 1) * ROWS] for j in range(X)]
            old = mx[h, :, lanes]
            m = old
            for j in range(X):
                m = jnp.maximum(m, jnp.max(blocks[j], axis=0, keepdims=True) - biases[j])
            factor = jnp.exp2(old - m)
            p = jnp.concatenate([jnp.exp2(blocks[j] - (m + biases[j])).astype(BF16) for j in range(X)], axis=0)
            values = jnp.concatenate([buf[slot, 1, h] for slot in slots], axis=1)
            values = jnp.concatenate([values, more_ones], axis=0)
            acc[h, :, lanes] = acc[h, :, lanes] * factor + jnp.dot(values, p, preferred_element_type=F32)
            mx[h, :, lanes] = m

    def step(t, carry):
        def dispatch(kind, low, high):
            if high - low > 1:
                middle = (low + high) // 2
                return lax.cond(
                    t < middle, lambda: dispatch(kind, low, middle), lambda: dispatch(kind, middle, high)
                )
            passed, group = PLAN[kind][low]
            with jax.named_scope(f"step{low}"):
                for dz, dx in passed:
                    arrived(kind, dz, dx, pieces(kind, dz, dx))
                    for piece, to in routes(kind, dz, dx):
                        copy(kind, dz, dx, piece, to).start()
            with jax.named_scope(f"sib{low}"):
                for of, dz, dx in group:
                    if of != kind:
                        arrived(of, dz, dx, "b")
            return tuple(jnp.int32(slot_of(*block)) for block in group)

        slots = lax.cond(core == 0, lambda: dispatch(0, 0, 16), lambda: dispatch(1, 0, 16))
        biases = []
        for slot in slots:
            of, dz, dx = slot // (Z * X), lax.rem(slot // X, Z), lax.rem(slot, X)
            seq = ord_ref[(lax.rem(z + dz, Z) * X + lax.rem(x + dx, X)) * 2 + of]
            biases.append(jnp.where((seq >= first_seq) & (seq < own_seq), 0.0, FAR))
        with jax.named_scope("attend"):
            attend(slots, biases)
        return carry

    lax.fori_loop(0, 16, step, 0)

    with jax.named_scope("attended"):
        for h in range(HKV):
            for g in range(GROUP):
                lanes = slice(g * ROWS, (g + 1) * ROWS)
                a = acc[h, 0:HEAD, lanes] / acc[h, HEAD : HEAD + 1, lanes]
                i = h * GROUP + g
                att[:, i * HEAD : (i + 1) * HEAD] = a.T.astype(BF16)

    own, above, below, over = tp, up[1], down[1], lax.rem(tp + 2, TP)
    half = NCHUNK // 2
    chunks = [n // 2 + (n % 2) * half for n in range(NCHUNK)]

    def y_copy(src, dst, index, target):
        return pltpu.make_async_remote_copy(
            src_ref=src, dst_ref=dst, send_sem=y_send, recv_sem=y_recv.at[index],
            device_id=target, device_id_type=MESH_ID,
        )

    def relay(n):
        return y_copy(part.at[n, over], rin.at[n], n, up if n < half else down)

    def direct(n):
        if n < half:
            return y_copy(part.at[n, below], right_in.at[n], NCHUNK + n, down)
        return y_copy(part.at[n, above], left_in.at[n], NCHUNK + n, up)

    def summed(n):
        if n < half:
            return y_copy(sums.at[n], left_in.at[n], 2 * NCHUNK + n, up)
        return y_copy(sums.at[n], right_in.at[n], 2 * NCHUNK + n, down)

    with jax.named_scope("project"):
        attended = att[...]
        ready = None
        for n in chunks:
            weights[n].wait()
            piece = jnp.dot(attended, wbuf[:, n * COLS : (n + 1) * COLS], preferred_element_type=F32)
            part[n] = piece.astype(BF16).reshape(TP, ROWS // TP, COLS)
            if ready is not None:
                relay(ready).start()
                direct(ready).start()
            ready = n
        relay(ready).start()
        direct(ready).start()
        ready = None
        for n in chunks:
            relay(n).wait_recv()
            onward = above if n < half else below
            sums[n] = (rin[n].astype(F32) + part[n, onward].astype(F32)).astype(BF16)
            if ready is not None:
                summed(ready).start()
            ready = n
        summed(ready).start()
        outs = []
        for n in chunks:
            direct(n).wait_recv()
            summed(n).wait_recv()
            total = part[n, own].astype(F32) + left_in[n].astype(F32) + right_in[n].astype(F32)
            outv[:, n * COLS : (n + 1) * COLS] = total.astype(BF16)
            outs.append(
                pltpu.make_async_copy(
                    outv.at[:, n * COLS : (n + 1) * COLS], out_ref.at[:, n * COLS : (n + 1) * COLS], w_sem.at[n]
                )
            )
            outs[-1].start()

    sent = part.at[0 : 3 * NCHUNK // TP]
    y = pltpu.make_async_remote_copy(
        src_ref=sent, dst_ref=sent, send_sem=y_send, recv_sem=y_recv.at[0], device_id=up, device_id_type=MESH_ID
    )
    y.wait_send()
    sent = buf.at[0 : 2 * Z * X - 1]
    blocks = pltpu.make_async_remote_copy(
        src_ref=sent, dst_ref=sent, send_sem=send, recv_sem=recv.at[0], device_id=at("s"), device_id_type=MESH_ID
    )
    blocks.wait_send()
    for c in outs:
        c.wait()


def local(queries, keys, values, doc_blocks, block_order, out_weight):
    any_, smem = pl.BlockSpec(memory_space=pl.ANY), pl.BlockSpec(memory_space=pltpu.SMEM)
    rows = ROWS // TP
    return pl.pallas_call(
        kernel,
        out_shape=jax.ShapeDtypeStruct((rows, WIN), BF16),
        in_specs=[any_, any_, any_, smem, smem, any_],
        out_specs=any_,
        scratch_shapes=[
            pltpu.VMEM((2 * Z * X, 2, HKV, ROWS, HEAD), BF16),
            pltpu.VMEM((ROWS, HKV * GROUP * HEAD), BF16),
            pltpu.VMEM((ROWS, HKV * HEAD), BF16),
            pltpu.VMEM((HKV * GROUP * HEAD, WIN), BF16),
            pltpu.VMEM((HKV, 2 * HEAD, QL), BF16),
            pltpu.VMEM((HKV, HEAD + ONES, QL), F32),
            pltpu.VMEM((HKV, 1, QL), F32),
            pltpu.VMEM((ROWS, HKV * GROUP * HEAD), BF16),
            pltpu.VMEM((NCHUNK, TP, rows, COLS), BF16),
            pltpu.VMEM((NCHUNK, rows, COLS), BF16),
            pltpu.VMEM((NCHUNK, rows, COLS), BF16),
            pltpu.VMEM((NCHUNK, rows, COLS), BF16),
            pltpu.VMEM((NCHUNK, rows, COLS), BF16),
            pltpu.VMEM((rows, WIN), BF16),
            pltpu.SemaphoreType.DMA((2 * Z * X,)),
            pltpu.SemaphoreType.DMA((1 + Z,)),
            pltpu.SemaphoreType.DMA(()),
            pltpu.SemaphoreType.DMA(()),
            pltpu.SemaphoreType.DMA((3 * NCHUNK,)),
            pltpu.SemaphoreType.DMA((4,)),
            pltpu.SemaphoreType.DMA((NCHUNK,)),
        ],
        compiler_params=pltpu.CompilerParams(
            collective_id=0, has_side_effects=True, vmem_limit_bytes=60 * 1024 * 1024
        ),
        name="attention",
    )(queries, keys, values, doc_blocks, block_order, out_weight)


def solution(mesh):
    placed = (P("cp", "tp"), P("cp", "tp"), P("cp", "tp"), P(), P(), P("tp", None))
    return jax.shard_map(
        local, mesh=mesh, in_specs=placed, out_specs=P(("cp", "tp"), None), check_vma=False
    )
```

time: 68.6 us -> 62.2 us (0.907)
  Pallas kernels: 66.8 us -> 60.4 us
    pallas_call x1, Pallas kernels: 66.8 us -> 60.4 us  [local(): pl.pallas_call(kernel, out_shape=jax.ShapeDtypeStruct((rows, WIN), BF16),...]
where the time goes in v3:
time: 62.2 us; the launch traced here: 62.1 us
  Pallas kernels  60.4 us (97%)
  local copies, waits for them, and re-layouts  1.67 us (3%)
    pallas_call x1, Pallas kernels, local(): pl.pallas_call(kernel, out_shape=jax.ShapeDtypeStruct((rows, WIN), BF16),...  60.4 us
    unnamed x1, local copies, waits for them, and re-layouts  1.67 us

profile of v3, /device:TPU:1, one launch (start us, length us, event | category | flops | bytes accessed | tf_op | source)
XLA Modules:
  0.0 62.1 jit_solution(16568484708132262300)
XLA Ops:
  0.0 60.4 %attention.1 = bf16[32,4096]{1,0:T(8,128)(2,1)} custom-call(bf16[128,2048]{1,0:T(8,128)(2,1)} %q_ref.1, bf16[128,256]{1,0:T(8,128)(2,1)} %k_ref.1, bf16[128,256]{1,0:T(8,128)(2,1)} %v_ref.1, s32[4]{0:T(128)} %doc_ref.1, s32[64]{0:T(128)} %ord_ref.1, bf16[2048,4096]{1,0:T(8,128)(2,1)} %w_ref.1), custom_call_target="tpu_custom_call" | custom-call | tf_op jit(solution)/shard_map/attention/pallas_call | solution.py:354
  60.4 1.7 %copy.8 = bf16[32,4096]{1,0:T(8,128)(2,1)} copy(bf16[32,4096]{1,0:T(8,128)(2,1)} %attention.1) | data formatting | bytes 524288

commit v4 on v3

--- a/solution.py
+++ b/solution.py
@@ -13,7 +13,7 @@
 ROWS, HEAD, HKV, GROUP = 128, 128, 2, 8
 QL = GROUP * ROWS
 WIN = 4096
-TILE = 256
+TILE = 512
 NCHUNK, COLS = 8, 512
 ONES = 16
 FAR = 1e30
@@ -26,35 +26,35 @@
         ((), ((0, 0, -1), (0, 0, 1), (1, -1, 0), (1, 1, 0))),
         (((0, 2), (-2, 0), (2, 0)), ((1, 0, -1), (1, 0, 1), (0, 0, 2), (0, -2, 0))),
         (((-1, -1), (1, -1)), ((0, 2, 0), (1, -1, -1), (1, -1, 1), (0, -1, -1))),
-        (((-1, 1), (1, 1)), ((0, 1, -1), (1, -2, 0), (1, 2, 0), (1, 1, -1))),
-        ((), ((1, 1, 1), (0, -1, 1), (0, 1, 1), (1, 0, 2))),
+        ((), ((0, 1, -1), (1, -2, 0), (1, 2, 0), (1, 1, -1))),
+        (((-1, 1), (1, 1)), ((1, 1, 1), (1, 0, 2), (0, -1, 1), (0, 1, 1))),
         (((-1, 2), (1, 2)), ((1, -1, 2), (1, -2, -1), (1, -2, 1), (0, -1, 2))),
-        (((-3, 0), (3, 0)), ((0, 1, 2), (1, -3, 0), (1, 3, 0), (1, 2, -1))),
-        (((-2, -1), (2, -1)), ((1, 2, 1), (0, -3, 0), (0, 3, 0), (1, 1, 2))),
-        (((-2, 1), (2, 1)), ((1, -2, 2), (0, -2, -1), (0, 2, -1), (0, -2, 1))),
-        (((-2, 2), (2, 2)), ((0, 2, 1), (1, 4, 0), (1, -3, -1), (1, -3, 1))),
-        (((4, 0),), ((0, -2, 2), (0, 2, 2), (1, 3, -1), (1, 3, 1))),
-        (((-3, -1), (3, -1)), ((1, 2, 2), (0, 4, 0), (0, -3, -1), (0, 3, -1))),
-        (((-3, 1), (3, 1)), ((1, 4, -1), (1, 4, 1), (1, -3, 2), (0, -3, 1))),
-        (((-3, 2), (3, 2), (4, -1), (4, 1)), ((0, 3, 1), (1, 3, 2), (0, -3, 2), (0, 3, 2))),
-        (((4, 2),), ((0, 4, -1), (0, 4, 1), (1, 4, 2), (0, 4, 2))),
+        ((), ((0, 1, 2), (1, -3, 0), (1, 3, 0), (1, 2, -1))),
+        (((-3, 0), (3, 0)), ((1, 2, 1), (1, 1, 2), (0, -3, 0), (0, 3, 0))),
+        (((-2, -1), (2, -1)), ((1, -2, 2), (0, -2, -1), (0, 2, -1), (1, 4, 0))),
+        (((-2, 1), (2, 1)), ((1, -3, -1), (1, -3, 1), (0, -2, 1), (0, 2, 1))),
+        (((-2, 2), (2, 2), (4, 0)), ((1, 3, -1), (0, -2, 2), (0, 2, 2), (0, 4, 0))),
+        ((), ((1, 3, 1), (1, 2, 2), (1, 4, -1), (1, 4, 1))),
+        (((-3, -1), (3, -1), (-3, 1), (3, 1)), ((1, -3, 2), (0, -3, -1), (0, 3, -1), (0, -3, 1))),
+        (((-3, 2), (3, 2)), ((0, 3, 1), (1, 3, 2), (1, 4, 2), (0, -3, 2))),
+        (((4, -1), (4, 1), (4, 2)), ((0, 3, 2), (0, 4, -1), (0, 4, 1), (0, 4, 2))),
     ),
     (
         (((-1, 0), (1, 0), (0, -1), (0, 1)), ((0, 0, 0), (1, -1, 0), (1, 1, 0), (1, 0, 0))),
         ((), ((1, 0, -1), (1, 0, 1), (0, -1, 0), (0, 1, 0))),
         (((-1, -1), (-1, 1)), ((0, 0, -1), (0, 0, 1), (1, -1, -1), (1, -1, 1))),
         (((-2, 0), (2, 0), (1, -1), (1, 1)), ((0, 0, 2), (1, -2, 0), (1, 2, 0), (1, 1, -1))),
-        (((0, 2), (-1, 2)), ((1, 1, 1), (0, -2, 0), (0, 2, 0), (1, 0, 2))),
-        (((-2, -1), (-2, 1)), ((1, -1, 2), (0, -1, -1), (0, 1, -1), (1, -2, -1))),
+        (((0, 2),), ((1, 1, 1), (0, -2, 0), (0, 2, 0), (1, 0, 2))),
+        (((-1, 2), (-2, -1), (-2, 1)), ((0, -1, -1), (0, 1, -1), (1, -1, 2), (1, -2, -1))),
         (((-3, 0), (3, 0), (2, -1), (2, 1)), ((1, -2, 1), (0, -1, 1), (0, 1, 1), (1, -3, 0))),
-        (((1, 2), (-2, 2)), ((1, 3, 0), (1, 2, -1), (1, 2, 1), (1, 1, 2))),
-        ((), ((1, -2, 2), (0, -1, 2), (0, 1, 2), (0, -3, 0))),
-        (((4, 0), (-3, -1), (-3, 1), (3, -1), (3, 1)), ((0, 3, 0), (0, -2, -1), (1, 4, 0), (1, -3, -1))),
-        (((2, 2),), ((1, -3, 1), (1, 3, -1), (1, 3, 1), (0, 2, -1))),
-        ((), ((0, -2, 1), (1, 2, 2), (0, 2, 1), (0, -2, 2))),
-        (((4, -1), (4, 1), (-3, 2)), ((0, 2, 2), (0, 4, 0), (1, 4, -1), (1, 4, 1))),
-        (((3, 2),), ((1, -3, 2), (0, -3, -1), (1, 3, 2), (0, 3, -1))),
-        (((4, 2),), ((0, -3, 1), (0, 3, 1), (1, 4, 2), (0, -3, 2))),
+        (((1, 2),), ((1, 3, 0), (1, 2, -1), (1, 2, 1), (1, 1, 2))),
+        (((-2, 2), (4, 0), (-3, -1), (-3, 1)), ((0, -1, 2), (0, 1, 2), (1, -2, 2), (1, 4, 0))),
+        ((), ((1, -3, -1), (1, -3, 1), (0, -3, 0), (0, 3, 0))),
+        (((3, -1), (3, 1), (2, 2)), ((0, -2, -1), (0, 2, -1), (1, 3, -1), (1, 3, 1))),
+        (((4, -1), (4, 1)), ((1, 2, 2), (0, -2, 1), (0, 2, 1), (1, 4, -1))),
+        (((-3, 2),), ((1, 4, 1), (0, -2, 2), (0, 2, 2), (1, -3, 2))),
+        (((3, 2), (4, 2)), ((0, 4, 0), (1, 3, 2), (1, 4, 2), (0, -3, -1))),
+        ((), ((0, 3, -1), (0, -3, 1), (0, 3, 1), (0, -3, 2))),
         ((), ((0, 3, 2), (0, 4, -1), (0, 4, 1), (0, 4, 2))),
     ),
 )
@@ -70,9 +70,9 @@
     elif kind == 0 and dz == 0:
         out = [("b", "z+"), ("b", "z-")] + turn
     elif kind == 0 and dz == 4:
-        out = wide if dx == 0 else turn
+        out = []
     elif kind == 0:
-        out = z_out if abs(dz) < 3 or dx == 0 else []
+        out = z_out
     else:
         out = z_out + wide if dx == 0 else turn
     return out + [("b", "s")]
@@ -80,7 +80,7 @@
 
 def pieces(kind, dz, dx):
     if kind == 0:
-        return "kv" if dx == 2 and dz in (0, 4) or (dz, dx) == (4, 0) else "b"
+        return "kv" if dz == 4 or (dz, dx) == (0, 2) else "b"
     return "kv" if dx == 2 or (dz, dx) == (4, 0) else "b"
 
 
@@ -90,13 +90,13 @@
 
 def second_sem(kind, dz, dx):
     if kind == 0:
-        return {(0, 2): 0, (4, 0): 1, (4, 2): 2}[dz, dx]
+        return 4 if dz == 0 else dx % X
     return 0 if dx == 0 else 1 + dz % Z
 
 
 def kernel(
-    q_ref, k_ref, v_ref, doc_ref, ord_ref, w_ref, out_ref,
-    buf, qin, vin, wbuf, qt, acc, mx, att, part, rin, sums, left_in, right_in, outv,
+    q_ref, k_ref, v_ref, doc_ref, ord_ref, w_ref, own_out, left_in, right_in,
+    buf, qin, vin, wbuf, qt, acc, mx, att, part, rin, sums,
     recv, recv2, send, y_send, y_recv, local, w_sem,
 ):
     cp, tp = lax.axis_index("cp"), lax.axis_index("tp")
@@ -219,23 +219,32 @@
                 preferred_element_type=F32,
             )
 
-        coming = scores(*tiles[0])
-        for n, (h, i) in enumerate(tiles):
-            s = coming
-            if n + 1 < len(tiles):
-                coming = scores(*tiles[n + 1])
+        def soft(s, h, i):
             lanes = slice(i * TILE, (i + 1) * TILE)
             blocks = [s[j * ROWS : (j + 1) * ROWS] for j in range(X)]
             old = mx[h, :, lanes]
             m = old
             for j in range(X):
                 m = jnp.maximum(m, jnp.max(blocks[j], axis=0, keepdims=True) - biases[j])
-            factor = jnp.exp2(old - m)
+            mx[h, :, lanes] = m
             p = jnp.concatenate([jnp.exp2(blocks[j] - (m + biases[j])).astype(BF16) for j in range(X)], axis=0)
+            return p, jnp.exp2(old - m)
+
+        def add(p, factor, h, i):
+            lanes = slice(i * TILE, (i + 1) * TILE)
             values = jnp.concatenate([buf[slot, 1, h] for slot in slots], axis=1)
             values = jnp.concatenate([values, more_ones], axis=0)
             acc[h, :, lanes] = acc[h, :, lanes] * factor + jnp.dot(values, p, preferred_element_type=F32)
-            mx[h, :, lanes] = m
+
+        coming, waiting = scores(*tiles[0]), None
+        for n, tile in enumerate(tiles):
+            s = coming
+            if n + 1 < len(tiles):
+                coming = scores(*tiles[n + 1])
+            if waiting is not None:
+                add(*waiting)
+            waiting = soft(s, *tile) + tile
+        add(*waiting)
 
     def step(t, carry):
         def dispatch(kind, low, high):
@@ -286,18 +295,24 @@
             device_id=target, device_id_type=MESH_ID,
         )
 
+    def cols(n):
+        return slice(n * COLS, (n + 1) * COLS)
+
+    def kept(n):
+        return pltpu.make_async_copy(part.at[n, own], own_out.at[:, cols(n)], w_sem.at[n])
+
     def relay(n):
         return y_copy(part.at[n, over], rin.at[n], n, up if n < half else down)
 
     def direct(n):
         if n < half:
-            return y_copy(part.at[n, below], right_in.at[n], NCHUNK + n, down)
-        return y_copy(part.at[n, above], left_in.at[n], NCHUNK + n, up)
+            return y_copy(part.at[n, below], right_in.at[:, cols(n)], NCHUNK + n, down)
+        return y_copy(part.at[n, above], left_in.at[:, cols(n)], NCHUNK + n, up)
 
     def summed(n):
         if n < half:
-            return y_copy(sums.at[n], left_in.at[n], 2 * NCHUNK + n, up)
-        return y_copy(sums.at[n], right_in.at[n], 2 * NCHUNK + n, down)
+            return y_copy(sums.at[n], left_in.at[:, cols(n)], 2 * NCHUNK + n, up)
+        return y_copy(sums.at[n], right_in.at[:, cols(n)], 2 * NCHUNK + n, down)
 
     with jax.named_scope("project"):
         attended = att[...]
@@ -309,9 +324,11 @@
             if ready is not None:
                 relay(ready).start()
                 direct(ready).start()
+                kept(ready).start()
             ready = n
         relay(ready).start()
         direct(ready).start()
+        kept(ready).start()
         ready = None
         for n in chunks:
             relay(n).wait_recv()
@@ -321,18 +338,9 @@
                 summed(ready).start()
             ready = n
         summed(ready).start()
-        outs = []
         for n in chunks:
             direct(n).wait_recv()
             summed(n).wait_recv()
-            total = part[n, own].astype(F32) + left_in[n].astype(F32) + right_in[n].astype(F32)
-            outv[:, n * COLS : (n + 1) * COLS] = total.astype(BF16)
-            outs.append(
-                pltpu.make_async_copy(
-                    outv.at[:, n * COLS : (n + 1) * COLS], out_ref.at[:, n * COLS : (n + 1) * COLS], w_sem.at[n]
-                )
-            )
-            outs[-1].start()
 
     sent = part.at[0 : 3 * NCHUNK // TP]
     y = pltpu.make_async_remote_copy(
@@ -344,18 +352,18 @@
         src_ref=sent, dst_ref=sent, send_sem=send, recv_sem=recv.at[0], device_id=at("s"), device_id_type=MESH_ID
     )
     blocks.wait_send()
-    for c in outs:
-        c.wait()
+    for n in range(NCHUNK):
+        kept(n).wait()
 
 
 def local(queries, keys, values, doc_blocks, block_order, out_weight):
     any_, smem = pl.BlockSpec(memory_space=pl.ANY), pl.BlockSpec(memory_space=pltpu.SMEM)
     rows = ROWS // TP
-    return pl.pallas_call(
+    own, left, right = pl.pallas_call(
         kernel,
-        out_shape=jax.ShapeDtypeStruct((rows, WIN), BF16),
+        out_shape=[jax.ShapeDtypeStruct((rows, WIN), BF16)] * 3,
         in_specs=[any_, any_, any_, smem, smem, any_],
-        out_specs=any_,
+        out_specs=[any_] * 3,
         scratch_shapes=[
             pltpu.VMEM((2 * Z * X, 2, HKV, ROWS, HEAD), BF16),
             pltpu.VMEM((ROWS, HKV * GROUP * HEAD), BF16),
@@ -368,9 +376,6 @@
             pltpu.VMEM((NCHUNK, TP, rows, COLS), BF16),
             pltpu.VMEM((NCHUNK, rows, COLS), BF16),
             pltpu.VMEM((NCHUNK, rows, COLS), BF16),
-            pltpu.VMEM((NCHUNK, rows, COLS), BF16),
-            pltpu.VMEM((NCHUNK, rows, COLS), BF16),
-            pltpu.VMEM((rows, WIN), BF16),
             pltpu.SemaphoreType.DMA((2 * Z * X,)),
             pltpu.SemaphoreType.DMA((1 + Z,)),
             pltpu.SemaphoreType.DMA(()),
@@ -384,6 +389,7 @@
         ),
         name="attention",
     )(queries, keys, values, doc_blocks, block_order, out_weight)
+    return (own.astype(F32) + left.astype(F32) + right.astype(F32)).astype(BF16)
 
 
 def solution(mesh):

time: 62.2 us -> 58.4 us (0.939)
  Pallas kernels: 60.4 us -> 56.4 us
  other arithmetic: 0 us -> 1.91 us
  local copies, waits for them, and re-layouts: 1.67 us -> 0 us
    pallas_call x1, Pallas kernels: 60.4 us -> 56.4 us  [local(): pl.pallas_call(kernel, out_shape=[jax.ShapeDtypeStruct((rows, WIN), BF16)...]
    convert_element_type x0 -> x1, other arithmetic: none -> 1.91 us  [local(): return (own.astype(F32) + left.astype(F32) + right.astype(F32)).astype(BF16)]
    unnamed x1 -> x0, local copies, waits for them, and re-layouts: 1.67 us -> none
where the time goes in v4:
time: 58.4 us; the launch traced here: 58.3 us
  Pallas kernels  56.4 us (97%)
  other arithmetic  1.91 us (3%)
    pallas_call x1, Pallas kernels, local(): pl.pallas_call(kernel, out_shape=[jax.ShapeDtypeStruct((rows, WIN), BF16)...  56.4 us
    convert_element_type x1, other arithmetic, local(): return (own.astype(F32) + left.astype(F32) + right.astype(F32)).astype(BF16)  1.91 us

profile of v4, /device:TPU:1, one launch (start us, length us, event | category | flops | bytes accessed | tf_op | source)
XLA Modules:
  0.0 58.3 jit_solution(19503498064025949)
XLA Ops:
  0.0 56.4 %attention.1 = (bf16[32,4096]{1,0:T(8,128)(2,1)}, bf16[32,4096]{1,0:T(8,128)(2,1)}, bf16[32,4096]{1,0:T(8,128)(2,1)}) custom-call(bf16[128,2048]{1,0:T(8,128)(2,1)} %q_ref.1, bf16[128,256]{1,0:T(8,128)(2,1)} %k_ref.1, bf16[128,256]{1,0:T(8,128)(2,1)} %v_ref.1, s32[4]{0:T(128)} %doc_ref.1, s32[64]{0:T(128)} %ord_ref.1, bf16[2048,4096]{1,0:T(8,128)(2,1)} %w_ref.1), custom_call_target="tpu_custom_call" | custom-call | tf_op jit(solution)/shard_map/attention/pallas_call | solution.py:362
  56.4 1.9 %add_convert_fusion = bf16[32,4096]{1,0:T(8,128)(2,1)} fusion(bf16[32,4096]{1,0:T(8,128)(2,1)} %get-tuple-element.10, bf16[32,4096]{1,0:T(8,128)(2,1)} %get-tuple-element.9, bf16[32,4096]{1,0:T(8,128)(2,1)} %get-tuple-element.8), kind=kLoop, calls=%fused_computation | loop fusion | flops 786432 | bytes 1048576 | tf_op jit(solution)/shard_map/convert_element_type | solution.py:392

commit v5 on v4

--- a/solution.py
+++ b/solution.py
@@ -27,15 +27,15 @@
         (((0, 2), (-2, 0), (2, 0)), ((1, 0, -1), (1, 0, 1), (0, 0, 2), (0, -2, 0))),
         (((-1, -1), (1, -1)), ((0, 2, 0), (1, -1, -1), (1, -1, 1), (0, -1, -1))),
         ((), ((0, 1, -1), (1, -2, 0), (1, 2, 0), (1, 1, -1))),
-        (((-1, 1), (1, 1)), ((1, 1, 1), (1, 0, 2), (0, -1, 1), (0, 1, 1))),
-        (((-1, 2), (1, 2)), ((1, -1, 2), (1, -2, -1), (1, -2, 1), (0, -1, 2))),
-        ((), ((0, 1, 2), (1, -3, 0), (1, 3, 0), (1, 2, -1))),
-        (((-3, 0), (3, 0)), ((1, 2, 1), (1, 1, 2), (0, -3, 0), (0, 3, 0))),
-        (((-2, -1), (2, -1)), ((1, -2, 2), (0, -2, -1), (0, 2, -1), (1, 4, 0))),
-        (((-2, 1), (2, 1)), ((1, -3, -1), (1, -3, 1), (0, -2, 1), (0, 2, 1))),
-        (((-2, 2), (2, 2), (4, 0)), ((1, 3, -1), (0, -2, 2), (0, 2, 2), (0, 4, 0))),
-        ((), ((1, 3, 1), (1, 2, 2), (1, 4, -1), (1, 4, 1))),
-        (((-3, -1), (3, -1), (-3, 1), (3, 1)), ((1, -3, 2), (0, -3, -1), (0, 3, -1), (0, -3, 1))),
+        (((-1, 1), (1, 1)), ((1, 1, 1), (1, 0, 2), (1, -1, 2), (0, -1, 1))),
+        (((-1, 2), (1, 2)), ((0, 1, 1), (1, -2, -1), (1, -2, 1), (0, -1, 2))),
+        (((-3, 0), (3, 0)), ((0, 1, 2), (1, -3, 0), (1, 3, 0), (0, -3, 0))),
+        ((), ((0, 3, 0), (1, 2, -1), (1, 2, 1), (1, 1, 2))),
+        (((-2, -1), (2, -1), (-2, 1), (2, 1)), ((1, -2, 2), (0, -2, -1), (0, 2, -1), (0, -2, 1))),
+        (((-2, 2), (2, 2)), ((0, 2, 1), (1, 4, 0), (1, -3, -1), (1, -3, 1))),
+        (((4, 0),), ((0, -2, 2), (0, 2, 2), (1, 3, -1), (1, 3, 1))),
+        (((-3, -1), (3, -1)), ((1, 2, 2), (0, 4, 0), (1, 4, -1), (1, 4, 1))),
+        (((-3, 1), (3, 1)), ((0, -3, -1), (0, 3, -1), (1, -3, 2), (0, -3, 1))),
         (((-3, 2), (3, 2)), ((0, 3, 1), (1, 3, 2), (1, 4, 2), (0, -3, 2))),
         (((4, -1), (4, 1), (4, 2)), ((0, 3, 2), (0, 4, -1), (0, 4, 1), (0, 4, 2))),
     ),
@@ -44,14 +44,14 @@
         ((), ((1, 0, -1), (1, 0, 1), (0, -1, 0), (0, 1, 0))),
         (((-1, -1), (-1, 1)), ((0, 0, -1), (0, 0, 1), (1, -1, -1), (1, -1, 1))),
         (((-2, 0), (2, 0), (1, -1), (1, 1)), ((0, 0, 2), (1, -2, 0), (1, 2, 0), (1, 1, -1))),
-        (((0, 2),), ((1, 1, 1), (0, -2, 0), (0, 2, 0), (1, 0, 2))),
-        (((-1, 2), (-2, -1), (-2, 1)), ((0, -1, -1), (0, 1, -1), (1, -1, 2), (1, -2, -1))),
-        (((-3, 0), (3, 0), (2, -1), (2, 1)), ((1, -2, 1), (0, -1, 1), (0, 1, 1), (1, -3, 0))),
-        (((1, 2),), ((1, 3, 0), (1, 2, -1), (1, 2, 1), (1, 1, 2))),
-        (((-2, 2), (4, 0), (-3, -1), (-3, 1)), ((0, -1, 2), (0, 1, 2), (1, -2, 2), (1, 4, 0))),
-        ((), ((1, -3, -1), (1, -3, 1), (0, -3, 0), (0, 3, 0))),
-        (((3, -1), (3, 1), (2, 2)), ((0, -2, -1), (0, 2, -1), (1, 3, -1), (1, 3, 1))),
-        (((4, -1), (4, 1)), ((1, 2, 2), (0, -2, 1), (0, 2, 1), (1, 4, -1))),
+        (((0, 2), (-1, 2)), ((1, 1, 1), (0, -2, 0), (0, 2, 0), (1, 0, 2))),
+        (((-2, -1), (-2, 1)), ((1, -1, 2), (0, -1, -1), (0, 1, -1), (1, -2, -1))),
+        (((-3, 0), (3, 0), (2, -1), (2, 1)), ((1, -2, 1), (1, -3, 0), (1, 3, 0), (1, 2, -1))),
+        (((1, 2), (-2, 2)), ((1, 2, 1), (0, -1, 1), (0, 1, 1), (1, 1, 2))),
+        ((), ((1, -2, 2), (0, -1, 2), (0, 1, 2), (0, -3, 0))),
+        (((4, 0), (-3, -1), (-3, 1)), ((0, 3, 0), (1, 4, 0), (1, -3, -1), (1, -3, 1))),
+        (((3, -1), (3, 1), (2, 2)), ((0, -2, -1), (1, 3, -1), (1, 3, 1), (1, 2, 2))),
+        (((4, -1), (4, 1)), ((0, 2, -1), (0, -2, 1), (0, 2, 1), (1, 4, -1))),
         (((-3, 2),), ((1, 4, 1), (0, -2, 2), (0, 2, 2), (1, -3, 2))),
         (((3, 2), (4, 2)), ((0, 4, 0), (1, 3, 2), (1, 4, 2), (0, -3, -1))),
         ((), ((0, 3, -1), (0, -3, 1), (0, 3, 1), (0, -3, 2))),
@@ -323,12 +323,12 @@
             part[n] = piece.astype(BF16).reshape(TP, ROWS // TP, COLS)
             if ready is not None:
                 relay(ready).start()
-                direct(ready).start()
                 kept(ready).start()
             ready = n
         relay(ready).start()
-        direct(ready).start()
         kept(ready).start()
+        for n in chunks:
+            direct(n).start()
         ready = None
         for n in chunks:
             relay(n).wait_recv()

time: 58.4 us -> 58.8 us (level)
  no operation moved by 1% of the time
where the time goes in v5:
time: 58.8 us; the launch traced here: 58.6 us
  Pallas kernels  56.7 us (96%)
  other arithmetic  1.91 us (3%)
    pallas_call x1, Pallas kernels, local(): pl.pallas_call(kernel, out_shape=[jax.ShapeDtypeStruct((rows, WIN), BF16)...  56.7 us
    convert_element_type x1, other arithmetic, local(): return (own.astype(F32) + left.astype(F32) + right.astype(F32)).astype(BF16)  1.91 us

profile of v5, /device:TPU:1, one launch (start us, length us, event | category | flops | bytes accessed | tf_op | source)
XLA Modules:
  0.0 58.6 jit_solution(12500575970436762729)
XLA Ops:
  0.0 56.7 %attention.1 = (bf16[32,4096]{1,0:T(8,128)(2,1)}, bf16[32,4096]{1,0:T(8,128)(2,1)}, bf16[32,4096]{1,0:T(8,128)(2,1)}) custom-call(bf16[128,2048]{1,0:T(8,128)(2,1)} %q_ref.1, bf16[128,256]{1,0:T(8,128)(2,1)} %k_ref.1, bf16[128,256]{1,0:T(8,128)(2,1)} %v_ref.1, s32[4]{0:T(128)} %doc_ref.1, s32[64]{0:T(128)} %ord_ref.1, bf16[2048,4096]{1,0:T(8,128)(2,1)} %w_ref.1), custom_call_target="tpu_custom_call" | custom-call | tf_op jit(solution)/shard_map/attention/pallas_call | solution.py:362
  56.7 1.9 %add_convert_fusion = bf16[32,4096]{1,0:T(8,128)(2,1)} fusion(bf16[32,4096]{1,0:T(8,128)(2,1)} %get-tuple-element.10, bf16[32,4096]{1,0:T(8,128)(2,1)} %get-tuple-element.9, bf16[32,4096]{1,0:T(8,128)(2,1)} %get-tuple-element.8), kind=kLoop, calls=%fused_computation | loop fusion | flops 786432 | bytes 1048576 | tf_op jit(solution)/shard_map/convert_element_type | solution.py:392

commit v6 on v4

--- a/solution.py
+++ b/solution.py
@@ -171,8 +171,6 @@
             for piece, to in routes(kind, 0, 0):
                 copy(kind, 0, 0, piece, to).start()
 
-    for c in weights:
-        c.start()
 
     with jax.named_scope("queries"):
         loads[3].wait()
@@ -271,6 +269,11 @@
             of, dz, dx = slot // (Z * X), lax.rem(slot // X, Z), lax.rem(slot, X)
             seq = ord_ref[(lax.rem(z + dz, Z) * X + lax.rem(x + dx, X)) * 2 + of]
             biases.append(jnp.where((seq >= first_seq) & (seq < own_seq), 0.0, FAR))
+        @pl.when(t == 2)
+        def _():
+            for c in weights:
+                c.start()
+
         with jax.named_scope("attend"):
             attend(slots, biases)
         return carry

time: 58.4 us -> 58.4 us (level)
  no operation moved by 1% of the time
where the time goes in v6:
time: 58.4 us; the launch traced here: 58.3 us
  Pallas kernels  56.4 us (97%)
  other arithmetic  1.91 us (3%)
    pallas_call x1, Pallas kernels, local(): pl.pallas_call(kernel, out_shape=[jax.ShapeDtypeStruct((rows, WIN), BF16)...  56.4 us
    convert_element_type x1, other arithmetic, local(): return (own.astype(F32) + left.astype(F32) + right.astype(F32)).astype(BF16)  1.91 us

profile of v6, /device:TPU:1, one launch (start us, length us, event | category | flops | bytes accessed | tf_op | source)
XLA Modules:
  0.0 58.3 jit_solution(10140775732241323220)
XLA Ops:
  0.0 56.4 %attention.1 = (bf16[32,4096]{1,0:T(8,128)(2,1)}, bf16[32,4096]{1,0:T(8,128)(2,1)}, bf16[32,4096]{1,0:T(8,128)(2,1)}) custom-call(bf16[128,2048]{1,0:T(8,128)(2,1)} %q_ref.1, bf16[128,256]{1,0:T(8,128)(2,1)} %k_ref.1, bf16[128,256]{1,0:T(8,128)(2,1)} %v_ref.1, s32[4]{0:T(128)} %doc_ref.1, s32[64]{0:T(128)} %ord_ref.1, bf16[2048,4096]{1,0:T(8,128)(2,1)} %w_ref.1), custom_call_target="tpu_custom_call" | custom-call | tf_op jit(solution)/shard_map/attention/pallas_call | solution.py:365
  56.4 1.9 %add_convert_fusion = bf16[32,4096]{1,0:T(8,128)(2,1)} fusion(bf16[32,4096]{1,0:T(8,128)(2,1)} %get-tuple-element.10, bf16[32,4096]{1,0:T(8,128)(2,1)} %get-tuple-element.9, bf16[32,4096]{1,0:T(8,128)(2,1)} %get-tuple-element.8), kind=kLoop, calls=%fused_computation | loop fusion | flops 786432 | bytes 1048576 | tf_op jit(solution)/shard_map/convert_element_type | solution.py:395
